TPU v7x, 128 devices: a whole 4x4x4 slice. The times are simulated.
128 devices in a mesh: dp: 8 (over y, core), mp: 16 (over x, z).
Axes of the slice: x: 4, y: 4, z: 4, core: 2. Of those that a mesh axis runs over, the one named last changes fastest.
Arguments:
- layer_input: bfloat16 [256, 256, 768], P(('dp', 'mp')), may hold values from -6 to 6
- output_cot: bfloat16 [256, 256, 768], P(('dp', 'mp')), may hold values from -6 to 6
- hidden_act: bfloat16 [256, 3072, 256], P('dp', 'mp'), may hold values from 0 to 2
- hidden_cot: bfloat16 [256, 3072, 256], P('dp', 'mp'), may hold values from -6 to 6
- lengths: int32 [256], P('dp'), may hold values from 32 to 256
- weights: float32 [768, 6144], P('dp', 'mp'), may hold values from -0.21875 to 0.21875
- moment_one: float32 [768, 6144], P('dp', 'mp'), may hold values from -3 to 3
- moment_two: float32 [768, 6144], P('dp', 'mp'), may hold values from 0.0005 to 0.02
Outputs:
- new_weights: float32 [768, 6144], P('dp', 'mp')
- new_moment_one: float32 [768, 6144], P('dp', 'mp')
- new_moment_two: float32 [768, 6144], P('dp', 'mp')
- clip_scale: float32 [256], P('dp')
Inputs may be any that keep to these rules, and one draw needn't show every extreme that they name: `lengths`: slots from an example's length on are padding.
All inputs are finite; a program needn't handle non-finite values.
Results may differ from a plain program's by a relative error of at most 0.0024.
Values may be sent and summed in bfloat16 or wider, within the bound.
A program may use at most 128 MiB of HBM per device.

v0:
```python
import math

import jax
import jax.numpy as jnp
from jax import lax
from jax.sharding import PartitionSpec as P

D = 768
FF = 3072
SLOT = 256
STEP = 10


beta_one = 0.9
beta_two = 0.999
adam_eps = 1e-08
learn_rate = 0.001
weight_decay = 0.01


def in_one_piece(arrays, axis, dim, along):
    both = jnp.concatenate(arrays, axis=along)
    result, at, finished = (lax.all_gather(both, axis, axis=dim, tiled=True), 0, [])
    for a in arrays:
        finished.append(lax.slice_in_dim(result, at, at + a.shape[along], axis=along))
        at += a.shape[along]
    return tuple(finished)


def from_everyone(value, axis):
    size = lax.axis_size(axis)
    return lax.all_to_all(
        jnp.broadcast_to(value[None], (size, *value.shape)), axis, 0, 0, tiled=True
    )


def taken_together(value, axis):
    everything = from_everyone(value, axis)
    return jnp.sum(everything, axis=0)


def in_blocks(value, dim, size):
    dims = value.shape
    tiles = value.reshape(*dims[:dim], size, dims[dim] // size, *dims[dim + 1 :])
    return jnp.moveaxis(tiles, dim, 0)


def sum_at_owner(value, axis, dim):
    size = lax.axis_size(axis)
    tiles = lax.all_to_all(in_blocks(value, dim, size), axis, 0, 0, tiled=True)
    return jnp.sum(tiles.astype(jnp.float32), axis=0)


def squared_norms(input_rows, outcot_rows, cot_rows, hid_rows):
    input_gram = jnp.einsum(
        "esd,etd->est", input_rows, input_rows, preferred_element_type=jnp.float32
    )
    cot_gram = jnp.einsum("efs,eft->est", cot_rows, cot_rows, preferred_element_type=jnp.float32)
    outcot_gram = jnp.einsum(
        "esd,etd->est", outcot_rows, outcot_rows, preferred_element_type=jnp.float32
    )
    hid_gram = jnp.einsum("efs,eft->est", hid_rows, hid_rows, preferred_element_type=jnp.float32)
    return jnp.sum(input_gram * cot_gram + outcot_gram * hid_gram, axis=(1, 2))


def clip_factor(squares):
    clip_limit = 0.5 * math.sqrt(2.0 * D * FF * SLOT)
    return clip_limit / jnp.maximum(jnp.sqrt(squares), clip_limit)


def masked_rows(own_lengths, hidden_cot, hidden_act):
    slot_index = lax.broadcasted_iota(jnp.int32, (own_lengths.shape[0], SLOT), 1)
    token_mask = (slot_index < own_lengths[:, None]).astype(jnp.float32)
    cot_masked = (hidden_cot.astype(jnp.float32) * token_mask[:, None, :]).astype(jnp.bfloat16)
    hid_masked = (hidden_act.astype(jnp.float32) * token_mask[:, None, :]).astype(jnp.bfloat16)
    return (token_mask, cot_masked, hid_masked)


def scaled_rows(clip_scale, token_mask, hidden_cot, hidden_act):
    factor = clip_scale[:, None] * token_mask
    scaled_cot = (hidden_cot.astype(jnp.float32) * factor[:, None, :]).astype(jnp.bfloat16)
    scaled_hid = (hidden_act.astype(jnp.float32) * factor[:, None, :]).astype(jnp.bfloat16)
    return (scaled_cot, scaled_hid)


def gradient_rows(input_rows, outcot_rows, cot_rows, hid_rows, row_count):
    contract = (((0, 1), (0, 2)), ((), ()))
    first_part = lax.dot_general(input_rows, cot_rows, contract, preferred_element_type=jnp.float32)
    second_part = lax.dot_general(
        outcot_rows, hid_rows, contract, preferred_element_type=jnp.float32
    )
    unit_count = cot_rows.shape[1]
    return jnp.stack([first_part, second_part], axis=2).reshape(row_count, 2 * unit_count)


def local(
    layer_input, output_cot, hidden_act, hidden_cot, lengths, weights, moment_one, moment_two
):
    local_examples = lengths.shape[0]
    input_full, outcot_full = in_one_piece((layer_input, output_cot), "mp", 0, 1)
    token_mask, cot_masked, hid_masked = masked_rows(lengths, hidden_cot, hidden_act)
    partial_squares = squared_norms(input_full, outcot_full, cot_masked, hid_masked)
    squares = taken_together(partial_squares, "mp")
    clip_scale = clip_factor(squares)
    scaled_cot, scaled_hid = scaled_rows(clip_scale, token_mask, hidden_cot, hidden_act)
    summed = sum_at_owner(
        gradient_rows(
            input_full,
            outcot_full,
            scaled_cot,
            scaled_hid,
            D // lax.axis_size("dp") * lax.axis_size("dp"),
        ).astype(jnp.bfloat16),
        "dp",
        0,
    )
    gradient = summed / (local_examples * lax.axis_size("dp"))
    new_moment_one = beta_one * moment_one + (1.0 - beta_one) * gradient
    new_moment_two = beta_two * moment_two + (1.0 - beta_two) * gradient * gradient
    corr_one = 1.0 - beta_one**STEP
    corr_two = 1.0 - beta_two**STEP
    direction = new_moment_one / corr_one / (jnp.sqrt(new_moment_two / corr_two) + adam_eps)
    new_weights = weights - learn_rate * (direction + weight_decay * weights)
    return (new_weights, new_moment_one, new_moment_two, clip_scale)


def solution(mesh):
    return jax.shard_map(
        local,
        mesh=mesh,
        in_specs=(
            P(("dp", "mp"), None, None),
            P(("dp", "mp"), None, None),
            P("dp", "mp", None),
            P("dp", "mp", None),
            P("dp"),
            P("dp", "mp"),
            P("dp", "mp"),
            P("dp", "mp"),
        ),
        out_specs=(P("dp", "mp"), P("dp", "mp"), P("dp", "mp"), P("dp")),
        check_vma=False,
    )
```

profile of v0, /device:TPU:1, one launch (start us, length us, event | category | flops | bytes accessed | tf_op | source)
XLA Modules:
  0.0 256.4 jit_solution(8981781877514634152)
XLA Ops:
  7.2 0.0 copy-start.1
  7.2 0.0 all-gather.2.cloned.1.call-start
  7.2 2.8 %pad_maximum_fusion = bf16[2,512,768]{2,1,0:T(8,128)(2,1)} fusion(bf16[2,256,768]{2,1,0:T(8,128)(2,1)} %param.9, bf16[2,256,768]{2,1,0:T(8,128)(2,1)} %param.8), kind=kLoop, calls=%fused_computation.22 | loop fusion | flops 3145728 | bytes 3145728 | tf_op jit(solution)/shard_map/concatenate | solution.py:22
  10.0 0.0 all-gather.2.cloned.1.call-update
  10.0 0.7 fusion.52
  10.7 0.0 copy-done.1
  10.8 4.8 %fusion.15 = f32[32,256,256]{2,1,0:T(8,128)} fusion(bf16[32,192,256]{2,1,0:T(8,128)(2,1)S(1)} %copy-done.1, f32[32,256]{1,0:T(8,128)S(1)} %fusion.52), kind=kOutput, calls=%fused_computation.17 | convolution fusion | flops 810024960 | bytes 11567104 | tf_op jit(solution)/shard_map/efs,eft->est/dot_general | solution.py:58
  15.5 151.9 %all-gather.2.cloned.1.call-done = bf16[32,512,768]{2,1,0:T(8,128)(2,1)} async-done(((bf16[2,512,768]{2,1,0:T(8,128)(2,1)}), bf16[32,512,768]{2,1,0:T(8,128)(2,1)}) %all-gather.2.cloned.1.call-update) | async-done | bytes 25165840 | tf_op jit(solution)/shard_map/all_gather | solution.py:23
  167.5 13.2 %fusion.2 = f32[32,256,256]{2,1,0:T(8,128)} fusion(bf16[32,512,768]{2,1,0:T(8,128)(2,1)} %all-gather.2.cloned.1.call-done), kind=kOutput, calls=%fused_computation.2 | convolution fusion | flops 3221225472 | bytes 20971520 | tf_op jit(solution)/shard_map/esd,etd->est/dot_general | solution.py:59
  180.7 0.0 copy-start
  180.7 13.6 %fusion.6 = f32[32,256,256]{2,1,0:T(8,128)} fusion(bf16[32,512,768]{2,1,0:T(8,128)(2,1)} %all-gather.2.cloned.1.call-done), kind=kOutput, calls=%fused_computation.6 | convolution fusion | flops 3221225472 | bytes 20971520 | tf_op jit(solution)/shard_map/esd,etd->est/dot_general | solution.py:55
  194.3 0.0 copy-done
  194.3 0.0 copy-start.6
  194.3 9.6 %add_reduce_fusion = f32[32]{0:T(128)S(1)} fusion(f32[32,256,256]{2,1,0:T(8,128)} %fusion.2, f32[32,256,256]{2,1,0:T(8,128)} %fusion.6, f32[32,256,256]{2,1,0:T(8,128)} %fusion.15, bf16[32,192,256]{2,1,0:T(8,128)(2,1)S(1)} %copy-done, f32[32,256]{1,0:T(8,128)S(1)} %fusion.52), kind=kOutput, calls=%fused_computation.8 | convolution fusion | flops 818413568 | bytes 28344448 | tf_op jit(solution)/shard_map/efs,eft->est/dot_general | solution.py:62
  203.9 11.2 %all_to_all.11 = f32[16,1,32]{2,1,0:T(1,128)S(1)} all-to-all(f32[16,1,32]{2,1,0:T(1,128)S(1)} %broadcast_in_dim.2), channel_id=1, replica_groups=mesh['dp'=8,'mp'=16] {'mp'}, dimensions={0} | all-to-all | bytes 4096 | tf_op jit(solution)/shard_map/all_to_all | solution.py:32
  215.2 0.0 copy-done.6
  215.2 0.0 copy-start.7
  215.2 0.1 fusion.51
  215.3 0.0 copy-start.2
  215.3 7.3 %fusion.46 = bf16[768,192,1]{0,1,2:T(8,128)(2,1)S(1)} fusion(bf16[32,512,768]{2,1,0:T(8,128)(2,1)} %all-gather.2.cloned.1.call-done, bf16[32,192,256]{2,1,0:T(8,128)(2,1)S(1)} %copy-done, f32[32,256]{1,0:T(8,128)S(1)} %fusion.51), kind=kOutput, calls=%fused_computation.29 | convolution fusion | flops 2420785152 | bytes 16056320 | tf_op jit(solution)/shard_map/dot_general | solution.py:89
  222.6 0.0 copy-done.7
  222.6 0.0 copy-done.2
  222.7 7.2 %fusion.41 = bf16[768,192,1]{0,1,2:T(8,128)(2,1)S(1)} fusion(bf16[32,512,768]{2,1,0:T(8,128)(2,1)} %all-gather.2.cloned.1.call-done, bf16[32,192,256]{2,1,0:T(8,128)(2,1)S(1)} %copy-done.2, f32[32,256]{1,0:T(8,128)S(1)} %fusion.51), kind=kOutput, calls=%fused_computation.28 | convolution fusion | flops 2420785152 | bytes 16056320 | tf_op jit(solution)/shard_map/dot_general | solution.py:88
  229.9 0.0 copy-start.3
  229.9 0.0 copy-start.4
  229.9 0.0 copy-start.5
  229.9 0.1 pad_maximum_fusion.1
  230.0 0.6 copy.45
  230.6 0.7 convert_element_type.42
  231.4 0.5 copy.46
  231.9 16.7 %all_to_all.12 = bf16[8,96,384]{2,1,0:T(8,128)(2,1)S(1)} all-to-all(bf16[8,96,384]{2,1,0:T(8,128)(2,1)S(1)} %copy.46), channel_id=1, replica_groups=mesh['dp'=8,'mp'=16] {'dp'}, dimensions={0} | all-to-all | bytes 1179648 | tf_op jit(solution)/shard_map/all_to_all | solution.py:50
  248.6 0.1 convert_reduce_fusion
  248.6 0.0 copy-done.3
  248.7 0.0 copy-done.4
  248.7 0.0 copy-done.5
  248.7 0.8 multiply_subtract_fusion
  (3 shorter events, 0.0 us)
Async XLA Ops:
  7.2 3.6 %copy-start.1 = (bf16[32,192,256]{2,1,0:T(8,128)(2,1)S(1)}, bf16[32,192,256]{2,1,0:T(8,128)(2,1)}, u32[]{:S(2)}) copy-start(bf16[32,192,256]{2,1,0:T(8,128)(2,1)} %param.11) | copy-start | bytes 9437188
  7.2 160.3 %all-gather.2.cloned.1.call-start = ((), (), s32[]{:S(2)}) async-start(), calls=%async_computation.2 | async-start | bytes 26738688 | tf_op jit(solution)/shard_map/all_gather | solution.py:23
  180.7 13.6 %copy-start = (bf16[32,192,256]{2,1,0:T(8,128)(2,1)S(1)}, bf16[32,192,256]{2,1,0:T(8,128)(2,1)}, u32[]{:S(2)}) copy-start(bf16[32,192,256]{2,1,0:T(8,128)(2,1)} %param.10) | copy-start | bytes 9437188
  194.3 20.9 %copy-start.6 = (s32[32]{0:T(128)S(1)}, s32[32]{0:T(128)}, u32[]{:S(2)}) copy-start(s32[32]{0:T(128)} %param.12) | copy-start | bytes 388
  215.2 7.4 %copy-start.7 = (f32[32]{0:T(128)}, f32[32]{0:T(128)S(1)}, u32[]{:S(2)}) copy-start(f32[32]{0:T(128)S(1)} %maximum_divide_fusion) | copy-start | bytes 388
  215.3 7.4 %copy-start.2 = (bf16[32,192,256]{2,1,0:T(8,128)(2,1)S(1)}, bf16[32,192,256]{2,1,0:T(8,128)(2,1)}, u32[]{:S(2)}) copy-start(bf16[32,192,256]{2,1,0:T(8,128)(2,1)} %param.11) | copy-start | bytes 9437188
  229.9 18.8 %copy-start.3 = (f32[96,384]{1,0:T(8,128)S(1)}, f32[96,384]{1,0:T(8,128)}, u32[]{:S(2)}) copy-start(f32[96,384]{1,0:T(8,128)} %param.13) | copy-start | bytes 442372
  229.9 18.7 %copy-start.4 = (f32[96,384]{1,0:T(8,128)S(1)}, f32[96,384]{1,0:T(8,128)}, u32[]{:S(2)}) copy-start(f32[96,384]{1,0:T(8,128)} %param.14) | copy-start | bytes 442372
  229.9 18.7 %copy-start.5 = (f32[96,384]{1,0:T(8,128)S(1)}, f32[96,384]{1,0:T(8,128)}, u32[]{:S(2)}) copy-start(f32[96,384]{1,0:T(8,128)} %param.15) | copy-start | bytes 442372
Sparse Core Ops, SparseCore 0:
  10.2 157.2 all-gather.1
where the time goes:
time: 257 us; the launch traced here: 256 us
  waiting for transfers between devices  152 us (59%)
  matrix products  55.8 us (22%)
  blocking collectives  27.9 us (11%)
  between operations  14.2 us (6%)
  other arithmetic  4.57 us (2%)
    all_gather x1, waiting for transfers between devices, in_one_piece(): lax.all_gather(both, axis, axis=dim, tiled=True)  152 us
    all_to_all x1, blocking collectives, sum_at_owner(): tiles = lax.all_to_all(in_blocks(value, dim, size), axis, 0, 0, tiled=True)  16.7 us
    dot_general x1, matrix products, squared_norms(): jnp.einsum('esd,etd->est', input_rows, input_rows, preferred_element_type...  13.6 us
    dot_general x1, matrix products, squared_norms(): jnp.einsum('esd,etd->est', outcot_rows, outcot_rows, preferred_element_ty...  13.2 us
    all_to_all x1, blocking collectives, from_everyone(): lax.all_to_all(jnp.broadcast_to(value[None], (size, *value.shape)), axis,...  11.2 us
    dot_general x1, matrix products, squared_norms(): jnp.einsum('efs,eft->est', hid_rows, hid_rows, preferred_element_type=jnp...  9.6 us
    dot_general x1, matrix products, gradient_rows(): lax.dot_general(outcot_rows, hid_rows, contract, preferred_element_type=j...  7.34 us
    dot_general x1, matrix products, gradient_rows(): lax.dot_general(input_rows, cot_rows, contract, preferred_element_type=jn...  7.24 us
  transfers between devices with their start and end apart: 1, of which 1 were waited for; matrix products, arithmetic and copies ran while one was open for 2% of the time, Pallas kernels for 0%

commit v1 on v0

v1 whole, which is shorter than its diff:
```python
import math

import jax
import jax.numpy as jnp
from jax import lax
from jax.experimental import pallas as pl
from jax.experimental.pallas import tpu as pltpu
from jax.sharding import PartitionSpec as P

D = 768
FF = 3072
SLOT = 256
STEP = 10
EXAMPLES = 256
ROWS = 192
OWN = 96

beta_one = 0.9
beta_two = 0.999
adam_eps = 1e-08
learn_rate = 0.001
weight_decay = 0.01
clip_limit = 0.5 * math.sqrt(2.0 * D * FF * SLOT)

MESH = pl.DeviceIdType.MESH
BF16 = jnp.bfloat16
F32 = jnp.float32


def kernel(
    x0_ref, x1_ref, h0_ref, h1_ref, len_ref,
    grad_ref, clip_ref,
    xb, hb, rb, gacc, gs, gr, gpad, ys, yr, eb, lb, mt, ft, npart, nb,
    lsem, llen, sx, sxo, sr, sh, sho, slen, sxf, srf, sn, sg, sy,
    rx, rxo, rr, rh, rho, rlen, rn, rg, ry,
):
    dp, mp = lax.axis_index("dp"), lax.axis_index("mp")
    c, y = lax.rem(dp, 2), lax.div(dp, 2)
    x, z = lax.div(mp, 4), lax.rem(mp, 4)
    other = 1 - c
    mod4 = lambda v: lax.rem(v + 8, 4)
    g = c * z + (1 - c) * x
    a = c * x + (1 - c) * z
    mp_of = lambda gg, aa: (1 - c) * (gg * 4 + aa) + c * (aa * 4 + gg)

    def remote(src, dst, ssem, rsem, to_dp, to_mp):
        return pltpu.make_async_remote_copy(
            src_ref=src, dst_ref=dst, send_sem=ssem, recv_sem=rsem,
            device_id={"dp": to_dp, "mp": to_mp}, device_id_type=MESH,
        )

    x_refs, h_refs = (x0_ref, x1_ref), (h0_ref, h1_ref)
    SIGN = (1, -1)
    OFF = (0, 1, 3, 2)
    HALF = ((0, 1), (3, 2))

    def place(k):
        return (x, z) if k == 0 else (z, x)

    def mp_k(k, gg, aa):
        return gg * 4 + aa if k == 0 else aa * 4 + gg

    def h_slice(k, i, aa):
        return h_refs[k].at[i, aa] if k == 0 else h_refs[k].at[aa, i]

    def h_all(k, aa):
        return h_refs[k].at[:, aa] if k == 0 else h_refs[k].at[aa]

    def d_x(k, s, j):
        gk, ak = place(k)
        return remote(x_refs[k].at[j], xb.at[c, gk, j], sx.at[k, s, j], rx.at[c, s, j],
                      y * 2 + k, mp_k(k, mod4(gk + SIGN[s]), ak))

    def d_relay(k, s, n):
        gk, ak = place(k)
        i = mod4(gk + HALF[s][n])
        return remote(h_slice(k, i, mod4(ak + 2)), rb.at[c, s, n], sr.at[k, s, n], rr.at[c, s, n],
                      y * 2 + k, mp_k(k, gk, mod4(ak + SIGN[s])))

    def d_h(k, s, n):
        gk, ak = place(k)
        i = mod4(gk + OFF[n])
        aa = mod4(ak + SIGN[s])
        return remote(h_slice(k, i, aa), hb.at[c, i, :, ak], sh.at[k, s, n], rh.at[c, s, n],
                      y * 2 + k, mp_k(k, gk, aa))

    def d_own_remote(k):
        gk, ak = place(k)
        return (
            remote(x_refs[k], xb.at[c, gk], sxo, rxo, y * 2 + k, mp),
            remote(h_all(k, ak), hb.at[c, :, :, ak], sho, rho, y * 2 + k, mp),
        )

    def d_own_local(k):
        gk, ak = place(k)
        return (
            pltpu.make_async_copy(x_refs[k], xb.at[c, gk], lsem.at[0]),
            pltpu.make_async_copy(h_all(k, ak), hb.at[c, :, :, ak], lsem.at[1]),
        )

    d_len = remote(len_ref, lb.at[c], slen, rlen, y * 2 + other, mp)
    d_len_local = pltpu.make_async_copy(len_ref, lb.at[c], llen)

    def d_xf(cp, s):
        src = xb.at[cp, mod4(g - SIGN[s]), s]
        return remote(src, src, sxf.at[cp, s], rx.at[cp, 2, s], dp, mp_of(mod4(g + SIGN[s]), a))

    def d_rf(cp, s, n):
        i = mod4(g + HALF[s][n])
        return remote(rb.at[cp, s, n], hb.at[cp, i, :, mod4(a - SIGN[s])], srf.at[cp, s, n],
                      rh.at[cp, 2, s * 2 + n], dp, mp_of(g, mod4(a + SIGN[s])))

    def w_x(cp, s, j):
        ref = xb.at[cp, mod4(g - SIGN[s]), j]
        remote(ref, ref, sx.at[0, s, j], rx.at[cp, s, j], dp, mp).wait_recv()

    def w_xf(cp, s):
        ref = xb.at[cp, mod4(g + 2), s]
        remote(ref, ref, sxf.at[0, s], rx.at[cp, 2, s], dp, mp).wait_recv()

    def w_relay(cp, s, n):
        ref = rb.at[cp, s, n]
        remote(ref, ref, sr.at[0, s, n], rr.at[cp, s, n], dp, mp).wait_recv()

    def w_h(cp, s, n):
        ref = hb.at[cp, mod4(g + OFF[n]), :, mod4(a - SIGN[s])]
        remote(ref, ref, sh.at[0, s, n], rh.at[cp, s, n], dp, mp).wait_recv()

    def w_hf(cp, s, n):
        ref = hb.at[cp, mod4(g + HALF[s][n]), :, mod4(a + 2)]
        remote(ref, ref, srf.at[0, s, n], rh.at[cp, 2, s * 2 + n], dp, mp).wait_recv()

    d_len_local.start()
    d_len.start()
    for k in range(2):
        @pl.when(c == k)
        def _():
            for d in d_own_local(k):
                d.start()

        @pl.when(c != k)
        def _():
            for d in d_own_remote(k):
                d.start()
    for q in range(2):
        for k in range(2):
            for s in range(2):
                d_x(k, s, q if s == 0 else 1 - q).start()
    for n in range(2):
        for k in range(2):
            for s in range(2):
                d_relay(k, s, n).start()

    f_row = lax.broadcasted_iota(jnp.int32, (256, 2 * ROWS), 0)
    column = lax.broadcasted_iota(jnp.int32, (256, 2 * ROWS), 1)
    for k in range(2):
        eb[k] = jnp.where(column == 2 * f_row + k, 1.0, 0.0).astype(BF16)
    npart[...] = jnp.zeros_like(npart)
    gpad[...] = jnp.zeros_like(gpad)

    d_len_local.wait()
    d_len.wait_recv()
    e_row = lax.broadcasted_iota(jnp.int32, (16, 32), 0)
    e_lane = lax.broadcasted_iota(jnp.int32, (16, 32), 1)
    e_place, e_half = lax.rem(lax.div(e_row, 2), 4), lax.rem(e_row, 2)
    wanted = mp_of(e_place, a) * 2 + e_half
    lens = jnp.where(e_row < 8, lb[0], lb[1]).astype(F32)
    len_col = jnp.sum(jnp.where(e_lane == wanted, lens, 0.0), axis=1, keepdims=True)
    slot = lax.broadcasted_iota(jnp.int32, (16, SLOT), 1).astype(F32)
    mask = jnp.where(slot < len_col, 1.0, 0.0)
    for e in range(16):
        mt[e] = mask[e : e + 1]

    def tiles(cp, i, m):
        for j in range(2):
            e = cp * 8 + i * 2 + j
            h = hb[cp, i, j, m] * mt[e].astype(BF16)
            p = jnp.dot(h, xb[cp, i, j], preferred_element_type=F32)
            p = jnp.sum((p * p).reshape(ROWS // 8, 8, D), axis=0)
            part = p[:, :128]
            for n in range(1, D // 128):
                part = part + p[:, n * 128 : (n + 1) * 128]
            npart[e] += part

    def loop(count, body):
        lax.fori_loop(0, count, lambda n, carry: (body(n), carry)[1], 0)

    for k in range(2):
        @pl.when(c == k)
        def _():
            for d in d_own_local(k):
                d.wait()
    own_x, own_h = xb.at[other, g], hb.at[other, :, :, a]
    remote(own_x, own_x, sxo, rxo, dp, mp).wait_recv()
    remote(own_h, own_h, sho, rho, dp, mp).wait_recv()

    for cp in range(2):
        for s in range(2):
            w_x(cp, s, s)
            d_xf(cp, s).start()
    for n in range(4):
        for k in range(2):
            for s in range(2):
                d_h(k, s, n).start()
    loop(2, lambda cp: tiles(cp, g, a))
    for cp in range(2):
        for s in range(2):
            w_x(cp, s, 1 - s)
    loop(4, lambda n: tiles(lax.div(n, 2), mod4(g + 1 + 2 * lax.rem(n, 2)), a))
    for n in range(2):
        for cp in range(2):
            for s in range(2):
                w_relay(cp, s, n)
                d_rf(cp, s, n).start()

    for n in range(3):
        for s in range(2):
            w_h(c, s, n)
        loop(2, lambda s: tiles(c, mod4(g + OFF[n]), mod4(a - 1 + 2 * s)))
    for cp in range(2):
        for s in range(2):
            w_xf(cp, s)
    loop(2, lambda cp: tiles(cp, mod4(g + 2), a))
    for s in range(2):
        w_h(c, s, 3)
    loop(2, lambda s: tiles(c, mod4(g + 2), mod4(a - 1 + 2 * s)))
    for n in range(4):
        for s in range(2):
            w_h(other, s, n)
        loop(2, lambda s: tiles(other, mod4(g + OFF[n]), mod4(a - 1 + 2 * s)))
        t, cp = n // 2, n % 2
        for s in range(2):
            w_hf(cp, s, t)
        loop(2, lambda s: tiles(cp, mod4(g + HALF[0][t] * (1 - s) + HALF[1][t] * s), mod4(a + 2)))

    spot = c * 16 + mp
    per_example = jnp.sum(npart[...], axis=1)
    col = jnp.sum(per_example, axis=1, keepdims=True)
    r16 = lax.broadcasted_iota(jnp.int32, (16, 128), 0)
    l16 = lax.broadcasted_iota(jnp.int32, (16, 128), 1)
    nb[spot] = jnp.sum(jnp.where(l16 == r16, col, 0.0), axis=0, keepdims=True)

    def d_norm(n):
        to = lax.rem(spot + n + 1, 32)
        return remote(nb.at[spot], nb.at[spot], sn.at[n], rn.at[spot],
                      y * 2 + lax.div(to, 16), lax.rem(to, 16))

    loop(31, lambda n: d_norm(n).start())

    def norm_wait(n):
        src = lax.rem(spot + n + 1, 32)
        remote(nb.at[src], nb.at[src], sn.at[n], rn.at[src], dp, mp).wait_recv()

    loop(31, norm_wait)
    rows = nb[...].reshape(32, 128)
    s0 = rows[0:4] + rows[4:8] + rows[8:12] + rows[12:16]
    s1 = jnp.concatenate(
        [jnp.sum(rows[16 + 4 * n : 20 + 4 * n], axis=0, keepdims=True) for n in range(4)], axis=0
    )

    def picked(table, index, shape):
        out = jnp.zeros(shape, F32)
        for n in range(4):
            out = out + jnp.where(index == n, table[n : n + 1], 0.0)
        return out

    def factor(squares):
        return clip_limit / jnp.maximum(jnp.sqrt(squares), clip_limit)

    mine = jnp.where(c == 0, s0, s1)
    others = jnp.where(c == 0, s1, s0)
    place16, half16 = lax.rem(lax.div(r16, 2), 4), lax.rem(r16, 2)
    squares = jnp.sum(
        jnp.where(l16 == r16, picked(mine, a, (16, 128)), 0.0)
        + jnp.where(l16 == lax.div(r16, 8) * 8 + a * 2 + half16, picked(others, place16, (16, 128)), 0.0),
        axis=1, keepdims=True,
    )
    scaled_mask = mask * factor(squares)
    for e in range(16):
        ft[e] = scaled_mask[e : e + 1]

    def block(m):
        for cp in range(2):
            total = None
            for i in range(4):
                for j in range(2):
                    h = (hb[cp, i, j, m].astype(F32) * ft[cp * 8 + i * 2 + j]).astype(BF16)
                    p = jnp.dot(h, xb[cp, i, j], preferred_element_type=F32)
                    total = p if total is None else total + p
            if cp == 0:
                gacc[...] = total
            else:
                gacc[...] += total

    def far(n):
        return 2 - n + 3 * (n // 2)

    def d_part(n):
        return remote(gs.at[n], gr.at[n], sg.at[n], rg.at[n], dp, mp_of(g, mod4(a + far(n))))

    def send_block(n):
        block(mod4(a + far(n)))
        gs[n] = gacc[...].astype(BF16)
        d_part(n).start()

    loop(3, send_block)
    block(a)

    r32 = lax.broadcasted_iota(jnp.int32, (32, 128), 0)
    l32 = lax.broadcasted_iota(jnp.int32, (32, 128), 1)
    x32, z32, j32 = lax.div(r32, 8), lax.rem(lax.div(r32, 2), 4), lax.rem(r32, 2)
    squares = jnp.sum(
        jnp.where(l32 == c * 8 + x32 * 2 + j32, picked(s0, z32, (32, 128)), 0.0)
        + jnp.where(l32 == c * 8 + z32 * 2 + j32, picked(s1, x32, (32, 128)), 0.0),
        axis=1, keepdims=True,
    )
    clip_ref[...] = jnp.sum(
        jnp.where(l32[:, :32] == r32[:, :32], factor(squares), 0.0), axis=0, keepdims=True
    )

    for n in range(3):
        remote(gr.at[n], gr.at[n], sg.at[n], rg.at[n], dp, mp).wait_recv()
    gpad[0:ROWS] = gacc[...] + gr[0].astype(F32) + gr[1].astype(F32) + gr[2].astype(F32)
    turned = gpad[...].T.astype(BF16)
    for b in range(8):
        ys[b] = turned[b * OWN : (b + 1) * OWN]

    def d_y(dy, k):
        to_y = mod4(y + dy)
        return remote(ys.at[to_y * 2 + k], yr.at[c, dy], sy.at[dy, k], ry.at[c, dy], to_y * 2 + k, mp)

    for dy in (2, 1, 3):
        for k in range(2):
            d_y(dy, k).start()
    d_partner = remote(ys.at[y * 2 + other], yr.at[c, 0], sy.at[0, 0], ry.at[c, 0], y * 2 + other, mp)
    d_partner.start()
    total = jnp.dot(ys[dp], eb[c], preferred_element_type=F32)
    remote(yr.at[other, 0], yr.at[other, 0], sy.at[0, 1], ry.at[other, 0], dp, mp).wait_recv()
    total = total + jnp.dot(yr[other, 0], eb[other], preferred_element_type=F32)
    for dy in (1, 3, 2):
        for k in range(2):
            remote(yr.at[k, dy], yr.at[k, dy], sy.at[dy, k], ry.at[k, dy], dp, mp).wait_recv()
            total = total + jnp.dot(yr[k, dy], eb[k], preferred_element_type=F32)
    grad_ref[...] = total * (1.0 / EXAMPLES)

    d_len.wait_send()
    for k in range(2):
        @pl.when(c != k)
        def _():
            for d in d_own_remote(k):
                d.wait_send()
        for s in range(2):
            for j in range(2):
                d_x(k, s, j).wait_send()
                d_relay(k, s, j).wait_send()
                d_rf(k, s, j).wait_send()
            for n in range(4):
                d_h(k, s, n).wait_send()
            d_xf(k, s).wait_send()
    loop(31, lambda n: d_norm(n).wait_send())
    for n in range(3):
        d_part(n).wait_send()
    for dy in (2, 1, 3):
        for k in range(2):
            d_y(dy, k).wait_send()
    d_partner.wait_send()


def exchange(layer_input, output_cot, hidden_cot, hidden_act, lengths):
    dma = pltpu.SemaphoreType.DMA
    hbm = pl.BlockSpec(memory_space=pltpu.HBM)
    vmem = pl.BlockSpec(memory_space=pltpu.VMEM)
    return pl.pallas_call(
        kernel,
        out_shape=(jax.ShapeDtypeStruct((OWN, 2 * ROWS), F32), jax.ShapeDtypeStruct((1, 32), F32)),
        in_specs=[hbm] * 5,
        out_specs=(vmem, vmem),
        scratch_shapes=[
            pltpu.VMEM((2, 4, 2, SLOT, D), BF16),
            pltpu.VMEM((2, 4, 2, 4, ROWS, SLOT), BF16),
            pltpu.VMEM((2, 2, 2, 2, ROWS, SLOT), BF16),
            pltpu.VMEM((ROWS, D), F32),
            pltpu.VMEM((3, ROWS, D), BF16),
            pltpu.VMEM((3, ROWS, D), BF16),
            pltpu.VMEM((256, D), F32),
            pltpu.VMEM((8, OWN, 256), BF16),
            pltpu.VMEM((2, 4, OWN, 256), BF16),
            pltpu.VMEM((2, 256, 2 * ROWS), BF16),
            pltpu.VMEM((2, 1, 32), jnp.int32),
            pltpu.VMEM((16, 1, SLOT), F32),
            pltpu.VMEM((16, 1, SLOT), F32),
            pltpu.VMEM((16, 8, 128), F32),
            pltpu.VMEM((32, 1, 128), F32),
            dma((2,)), dma, dma((2, 2, 2)), dma, dma((2, 2, 2)), dma((2, 2, 4)), dma, dma, dma((2, 2)),
            dma((2, 2, 2)), dma((31,)), dma((3,)), dma((4, 2)),
            dma((2, 3, 2)), dma, dma((2, 2, 2)), dma((2, 3, 4)), dma, dma, dma((32,)), dma((3,)), dma((2, 4)),
        ],
        compiler_params=pltpu.CompilerParams(has_side_effects=True, vmem_limit_bytes=60 * 1024 * 1024),
    )(layer_input, output_cot, hidden_cot, hidden_act, lengths)


def local(
    layer_input, output_cot, hidden_act, hidden_cot, lengths, weights, moment_one, moment_two
):
    by_place = (4, 4, 2, ROWS, SLOT)
    gradient, clip = exchange(
        layer_input, output_cot, hidden_cot.reshape(by_place), hidden_act.reshape(by_place), lengths.reshape(1, 32)
    )
    new_moment_one = beta_one * moment_one + (1.0 - beta_one) * gradient
    new_moment_two = beta_two * moment_two + (1.0 - beta_two) * gradient * gradient
    corr_one = 1.0 - beta_one**STEP
    corr_two = 1.0 - beta_two**STEP
    direction = new_moment_one / corr_one / (jnp.sqrt(new_moment_two / corr_two) + adam_eps)
    new_weights = weights - learn_rate * (direction + weight_decay * weights)
    return (new_weights, new_moment_one, new_moment_two, clip.reshape(32))


def solution(mesh):
    return jax.shard_map(
        local,
        mesh=mesh,
        in_specs=(
            P(("dp", "mp"), None, None),
            P(("dp", "mp"), None, None),
            P("dp", "mp", None),
            P("dp", "mp", None),
            P("dp"),
            P("dp", "mp"),
            P("dp", "mp"),
            P("dp", "mp"),
        ),
        out_specs=(P("dp", "mp"), P("dp", "mp"), P("dp", "mp"), P("dp")),
        check_vma=False,
    )
```

time: 257 us -> 107 us (0.42)
  waiting for transfers between devices: 152 us -> 0 us
  Pallas kernels: 0 us -> 103 us
  matrix products: 55.8 us -> 0 us
  blocking collectives: 27.9 us -> 0 us
  between operations: 14.2 us -> 0.69 us
  other arithmetic: 4.57 us -> 1.73 us
    all_gather x1 -> x0, waiting for transfers between devices: 152 us -> none  [in_one_piece(): lax.all_gather(both, axis, axis=dim, tiled=True)]
    pallas_call x0 -> x1, Pallas kernels: none -> 103 us  [exchange(): pl.pallas_call(kernel, out_shape=(jax.ShapeDtypeStruct((OWN, 2 * ROWS), F...]
    dot_general x6 -> x0, matrix products: 55.8 us -> none  [the longest x1 13.6 us: squared_norms(): jnp.einsum('esd,etd->est', input_rows, input_rows, preferred_element_type...]
    all_to_all x2 -> x0, blocking collectives: 27.9 us -> none  [the longest x1 16.7 us: sum_at_owner(): tiles = lax.all_to_all(in_blocks(value, dim, size), axis, 0, 0, tiled=True)]
    concatenate x1 -> x0, other arithmetic: 2.77 us -> none  [in_one_piece(): both = jnp.concatenate(arrays, axis=along)]
  transfers between devices with their start and end apart: 1 -> 0, of which waited for: 1 -> 0; matrix products, arithmetic and copies ran while one was open for 2% -> 0% of each run, Pallas kernels for 0% -> 0%
where the time goes in v1:
time: 107 us
  Pallas kernels  103 us (96%)
  other arithmetic  1.73 us (2%)
  local copies, waits for them, and re-layouts  1.13 us (1%)
    pallas_call x1, Pallas kernels, exchange(): pl.pallas_call(kernel, out_shape=(jax.ShapeDtypeStruct((OWN, 2 * ROWS), F...  103 us

profile of v1, /device:TPU:1, one launch (start us, length us, event | category | flops | bytes accessed | tf_op | source)
XLA Modules:
  0.0 106.5 jit_solution(12196164656208062138)
XLA Ops:
  0.6 0.0 copy-start
  0.6 0.0 copy-start.1
  0.7 0.0 copy-start.2
  0.7 103.0 %shard_map.111 = (f32[96,384]{1,0:T(8,128)}, f32[1,32]{1,0:T(1,128)}) custom-call(bf16[2,256,768]{2,1,0:T(8,128)(2,1)} %x0_ref.1, bf16[2,256,768]{2,1,0:T(8,128)(2,1)} %x1_ref.1, bf16[4,4,2,192,256]{4,3,2,1,0:T(8,128)(2,1)} %bitcast.4, bf16[4,4,2,192,256]{4,3,2,1,0:T(8,128)(2,1)} %bitcast.5, s32[1,32]{1,0:T(1,128)} %bitcast.6), custom_call_target="tpu_custom_call" | custom-call | tf_op jit(solution)/shard_map/pallas_call | solution.py:373
  103.6 0.0 copy-done
  103.7 0.0 copy-done.1
  103.7 0.0 copy-done.2
  103.7 1.7 %multiply_subtract_fusion = (f32[96,384]{1,0:T(8,128)}, f32[96,384]{1,0:T(8,128)}, f32[96,384]{1,0:T(8,128)}) fusion(f32[96,384]{1,0:T(8,128)S(1)} %copy-done, f32[96,384]{1,0:T(8,128)} %get-tuple-element.6, f32[96,384]{1,0:T(8,128)S(1)} %copy-done.1, f32[96,384]{1,0:T(8,128)S(1)} %copy-done.2), kind=kLoop, calls=%fused_computation.2 | loop fusion | flops 552960 | bytes 1032192 | tf_op jit(solution)/shard_map/sub | solution.py:414
  105.4 1.1 %copy.13 = f32[32]{0:T(128)} copy(f32[32]{0:T(128)} %bitcast.7) | data formatting | bytes 256
Async XLA Ops:
  0.6 103.0 %copy-start = (f32[96,384]{1,0:T(8,128)S(1)}, f32[96,384]{1,0:T(8,128)}, u32[]{:S(2)}) copy-start(f32[96,384]{1,0:T(8,128)} %param.13) | copy-start | bytes 442372
  0.6 103.0 %copy-start.1 = (f32[96,384]{1,0:T(8,128)S(1)}, f32[96,384]{1,0:T(8,128)}, u32[]{:S(2)}) copy-start(f32[96,384]{1,0:T(8,128)} %param.14) | copy-start | bytes 442372
  0.7 103.0 %copy-start.2 = (f32[96,384]{1,0:T(8,128)S(1)}, f32[96,384]{1,0:T(8,128)}, u32[]{:S(2)}) copy-start(f32[96,384]{1,0:T(8,128)} %param.15) | copy-start | bytes 442372

commit v2 on v1

--- a/solution.py
+++ b/solution.py
@@ -32,7 +32,7 @@
     grad_ref, clip_ref,
     xb, hb, rb, gacc, gs, gr, gpad, ys, yr, eb, lb, mt, ft, npart, nb,
     lsem, llen, sx, sxo, sr, sh, sho, slen, sxf, srf, sn, sg, sy,
-    rx, rxo, rr, rh, rho, rlen, rn, rg, ry,
+    rx, rxo, rr, rh, rho, rlen, rn, rg, ry, near,
 ):
     dp, mp = lax.axis_index("dp"), lax.axis_index("mp")
     c, y = lax.rem(dp, 2), lax.div(dp, 2)
@@ -130,6 +130,21 @@
         ref = hb.at[cp, mod4(g + HALF[s][n]), :, mod4(a + 2)]
         remote(ref, ref, srf.at[0, s, n], rh.at[cp, 2, s * 2 + n], dp, mp).wait_recv()
 
+    def signal(sem, to_dp, to_mp):
+        pl.semaphore_signal(sem, inc=1, device_id={"dp": to_dp, "mp": to_mp}, device_id_type=MESH)
+
+    in_x = [mod4(x + s) * 4 + z for s in SIGN]
+    in_z = [x * 4 + mod4(z + s) for s in SIGN]
+    in_y = [mod4(y + s) * 2 for s in SIGN]
+    barrier = pltpu.get_barrier_semaphore()
+    signal(barrier, y * 2 + other, mp)
+    for k in range(2):
+        for to_mp in in_x + in_z:
+            signal(barrier, y * 2 + k, to_mp)
+        for to_dp in in_y:
+            signal(barrier, to_dp + k, mp)
+    pl.semaphore_wait(barrier, 13)
+
     d_len_local.start()
     d_len.start()
     for k in range(2):
@@ -150,6 +165,11 @@
         for k in range(2):
             for s in range(2):
                 d_relay(k, s, n).start()
+
+    for to_mp in in_x:
+        signal(near.at[0], dp, to_mp)
+    for to_dp in in_y:
+        signal(near.at[0], to_dp + c, mp)
 
     f_row = lax.broadcasted_iota(jnp.int32, (256, 2 * ROWS), 0)
     column = lax.broadcasted_iota(jnp.int32, (256, 2 * ROWS), 1)
@@ -203,6 +223,9 @@
             for s in range(2):
                 d_h(k, s, n).start()
     loop(2, lambda cp: tiles(cp, g, a))
+    pl.semaphore_wait(near.at[0], 4)
+    for to_mp in in_z:
+        signal(near.at[1], dp, to_mp)
     for cp in range(2):
         for s in range(2):
             w_x(cp, s, 1 - s)
@@ -213,6 +236,10 @@
                 w_relay(cp, s, n)
                 d_rf(cp, s, n).start()
 
+    pl.semaphore_wait(near.at[1], 2)
+    for to_mp in in_z:
+        signal(near.at[2], dp, to_mp)
+
     for n in range(3):
         for s in range(2):
             w_h(c, s, n)
@@ -224,6 +251,7 @@
     for s in range(2):
         w_h(c, s, 3)
     loop(2, lambda s: tiles(c, mod4(g + 2), mod4(a - 1 + 2 * s)))
+    pl.semaphore_wait(near.at[2], 2)
     for n in range(4):
         for s in range(2):
             w_h(other, s, n)
@@ -394,8 +422,9 @@
             dma((2,)), dma, dma((2, 2, 2)), dma, dma((2, 2, 2)), dma((2, 2, 4)), dma, dma, dma((2, 2)),
             dma((2, 2, 2)), dma((31,)), dma((3,)), dma((4, 2)),
             dma((2, 3, 2)), dma, dma((2, 2, 2)), dma((2, 3, 4)), dma, dma, dma((32,)), dma((3,)), dma((2, 4)),
+            pltpu.SemaphoreType.REGULAR((3,)),
         ],
-        compiler_params=pltpu.CompilerParams(has_side_effects=True, vmem_limit_bytes=60 * 1024 * 1024),
+        compiler_params=pltpu.CompilerParams(has_side_effects=True, collective_id=0, vmem_limit_bytes=60 * 1024 * 1024),
     )(layer_input, output_cot, hidden_cot, hidden_act, lengths)
 
 

time: 107 us -> 99.7 us (0.932)
  Pallas kernels: 103 us -> 96 us
    pallas_call x1, Pallas kernels: 103 us -> 96 us  [exchange(): pl.pallas_call(kernel, out_shape=(jax.ShapeDtypeStruct((OWN, 2 * ROWS), F...]
where the time goes in v2:
time: 99.7 us; the launch traced here: 99.6 us
  Pallas kernels  96 us (96%)
  other arithmetic  1.73 us (2%)
  local copies, waits for them, and re-layouts  1.13 us (1%)
    pallas_call x1, Pallas kernels, exchange(): pl.pallas_call(kernel, out_shape=(jax.ShapeDtypeStruct((OWN, 2 * ROWS), F...  96 us

profile of v2, /device:TPU:1, one launch (start us, length us, event | category | flops | bytes accessed | tf_op | source)
XLA Modules:
  0.0 99.6 jit_solution(5741071521717296423)
XLA Ops:
  0.6 0.0 copy-start
  0.6 0.0 copy-start.1
  0.7 0.0 copy-start.2
  0.7 96.0 %shard_map.111 = (f32[96,384]{1,0:T(8,128)}, f32[1,32]{1,0:T(1,128)}) custom-call(bf16[2,256,768]{2,1,0:T(8,128)(2,1)} %x0_ref.1, bf16[2,256,768]{2,1,0:T(8,128)(2,1)} %x1_ref.1, bf16[4,4,2,192,256]{4,3,2,1,0:T(8,128)(2,1)} %bitcast.4, bf16[4,4,2,192,256]{4,3,2,1,0:T(8,128)(2,1)} %bitcast.5, s32[1,32]{1,0:T(1,128)} %bitcast.6), custom_call_target="tpu_custom_call" | custom-call | tf_op jit(solution)/shard_map/pallas_call | solution.py:401
  96.7 0.0 copy-done
  96.7 0.0 copy-done.1
  96.7 0.0 copy-done.2
  96.7 1.7 %multiply_subtract_fusion = (f32[96,384]{1,0:T(8,128)}, f32[96,384]{1,0:T(8,128)}, f32[96,384]{1,0:T(8,128)}) fusion(f32[96,384]{1,0:T(8,128)S(1)} %copy-done, f32[96,384]{1,0:T(8,128)} %get-tuple-element.6, f32[96,384]{1,0:T(8,128)S(1)} %copy-done.1, f32[96,384]{1,0:T(8,128)S(1)} %copy-done.2), kind=kLoop, calls=%fused_computation.2 | loop fusion | flops 552960 | bytes 1032192 | tf_op jit(solution)/shard_map/sub | solution.py:443
  98.4 1.1 %copy.13 = f32[32]{0:T(128)} copy(f32[32]{0:T(128)} %bitcast.7) | data formatting | bytes 256
Async XLA Ops:
  0.6 96.0 %copy-start = (f32[96,384]{1,0:T(8,128)S(1)}, f32[96,384]{1,0:T(8,128)}, u32[]{:S(2)}) copy-start(f32[96,384]{1,0:T(8,128)} %param.13) | copy-start | bytes 442372
  0.6 96.0 %copy-start.1 = (f32[96,384]{1,0:T(8,128)S(1)}, f32[96,384]{1,0:T(8,128)}, u32[]{:S(2)}) copy-start(f32[96,384]{1,0:T(8,128)} %param.14) | copy-start | bytes 442372
  0.7 96.0 %copy-start.2 = (f32[96,384]{1,0:T(8,128)S(1)}, f32[96,384]{1,0:T(8,128)}, u32[]{:S(2)}) copy-start(f32[96,384]{1,0:T(8,128)} %param.15) | copy-start | bytes 442372

commit v3 on v2

v3 whole, which is shorter than its diff:
```python
import math

import jax
import jax.numpy as jnp
from jax import lax
from jax.experimental import pallas as pl
from jax.experimental.pallas import tpu as pltpu
from jax.sharding import PartitionSpec as P

D = 768
FF = 3072
SLOT = 256
STEP = 10
EXAMPLES = 256
ROWS = 192
OWN = 96

beta_one = 0.9
beta_two = 0.999
adam_eps = 1e-08
learn_rate = 0.001
weight_decay = 0.01
clip_limit = 0.5 * math.sqrt(2.0 * D * FF * SLOT)

MESH = pl.DeviceIdType.MESH
BF16 = jnp.bfloat16
F32 = jnp.float32


def kernel(
    x0_ref, x1_ref, h0_ref, h1_ref, len_ref,
    grad_ref, clip_ref,
    xb, hb, gall, gs, gr, gpad, ys, yr, eb, lb, mt, ft, npart, nb,
    lsem, llen, sx, sxo, sh, sho, slen, sxf, sn, sg, sy,
    rx, rxo, rh, rho, rlen, rn, rg, ry, near,
):
    dp, mp = lax.axis_index("dp"), lax.axis_index("mp")
    c, y = lax.rem(dp, 2), lax.div(dp, 2)
    x, z = lax.div(mp, 4), lax.rem(mp, 4)
    other = 1 - c
    mod4 = lambda v: lax.rem(v + 8, 4)
    g = c * z + (1 - c) * x
    a = c * x + (1 - c) * z
    mp_of = lambda gg, aa: (1 - c) * (gg * 4 + aa) + c * (aa * 4 + gg)

    def remote(src, dst, ssem, rsem, to_dp, to_mp):
        return pltpu.make_async_remote_copy(
            src_ref=src, dst_ref=dst, send_sem=ssem, recv_sem=rsem,
            device_id={"dp": to_dp, "mp": to_mp}, device_id_type=MESH,
        )

    def signal(sem, to_dp, to_mp):
        pl.semaphore_signal(sem, inc=1, device_id={"dp": to_dp, "mp": to_mp}, device_id_type=MESH)

    def loop(count, body):
        lax.fori_loop(0, count, lambda n, carry: (body(n), carry)[1], 0)

    x_refs, h_refs = (x0_ref, x1_ref), (h0_ref, h1_ref)
    STEPS = (1, -1, 2)
    CHUNK = ROWS // 2

    def place(k):
        return (x, z) if k == 0 else (z, x)

    def mp_k(k, gg, aa):
        return gg * 4 + aa if k == 0 else aa * 4 + gg

    def h_slice(k, i, aa):
        return h_refs[k].at[i, aa] if k == 0 else h_refs[k].at[aa, i]

    def h_all(k, aa):
        return h_refs[k].at[:, aa] if k == 0 else h_refs[k].at[aa]

    def d_x(k, s, j):
        gk, ak = place(k)
        return remote(x_refs[k].at[j], xb.at[c, gk, j], sx.at[k, s, j], rx.at[c, s, j],
                      y * 2 + k, mp_k(k, mod4(gk + STEPS[s]), ak))

    def d_h(k, s, r):
        gk, ak = place(k)
        aa = mod4(ak + STEPS[s])
        i = mod4(r - aa)
        return remote(h_slice(k, i, aa), hb.at[c, i, :, ak], sh.at[k, s, r], rh.at[c, s, r],
                      y * 2 + k, mp_k(k, gk, aa))

    def d_own_remote(k):
        gk, ak = place(k)
        return (
            remote(x_refs[k], xb.at[c, gk], sxo, rxo, y * 2 + k, mp),
            remote(h_all(k, ak), hb.at[c, :, :, ak], sho, rho, y * 2 + k, mp),
        )

    def d_own_local(k):
        gk, ak = place(k)
        return (
            pltpu.make_async_copy(x_refs[k], xb.at[c, gk], lsem.at[0]),
            pltpu.make_async_copy(h_all(k, ak), hb.at[c, :, :, ak], lsem.at[1]),
        )

    d_len = remote(len_ref, lb.at[c], slen, rlen, y * 2 + other, mp)
    d_len_local = pltpu.make_async_copy(len_ref, lb.at[c], llen)

    def d_xf(cp, s):
        src = xb.at[cp, mod4(g - STEPS[s]), s]
        return remote(src, src, sxf.at[cp, s], rx.at[cp, 2, s], dp, mp_of(mod4(g + STEPS[s]), a))

    def w_x(cp, s, j):
        ref = xb.at[cp, mod4(g - STEPS[s]), j]
        remote(ref, ref, sx.at[0, s, j], rx.at[cp, s, j], dp, mp).wait_recv()

    def w_xf(cp, s):
        ref = xb.at[cp, mod4(g + 2), s]
        remote(ref, ref, sxf.at[0, s], rx.at[cp, 2, s], dp, mp).wait_recv()

    def w_h(cp, s, r):
        ref = hb.at[cp, mod4(r - a), :, mod4(a - STEPS[s])]
        remote(ref, ref, sh.at[0, s, r], rh.at[cp, s, r], dp, mp).wait_recv()

    in_x = [mod4(x + s) * 4 + z for s in STEPS[:2]]
    in_z = [x * 4 + mod4(z + s) for s in STEPS[:2]]
    in_y = [mod4(y + s) * 2 for s in STEPS[:2]]
    barrier = pltpu.get_barrier_semaphore()
    signal(barrier, y * 2 + other, mp)
    for k in range(2):
        for to_mp in in_x + in_z:
            signal(barrier, y * 2 + k, to_mp)
        for to_dp in in_y:
            signal(barrier, to_dp + k, mp)
    pl.semaphore_wait(barrier, 13)

    for q in range(2):
        for k in range(2):
            for s in range(2):
                d_x(k, s, q if s == 0 else 1 - q).start()
    d_len_local.start()
    d_len.start()
    for k in range(2):
        @pl.when(c == k)
        def _():
            for d in d_own_local(k):
                d.start()

        @pl.when(c != k)
        def _():
            for d in d_own_remote(k):
                d.start()
    for to_mp in in_x + in_z:
        signal(near.at[0], dp, to_mp)
    for to_dp in in_y:
        signal(near.at[0], to_dp + c, mp)

    f_row = lax.broadcasted_iota(jnp.int32, (128, 2 * ROWS), 0)
    column = lax.broadcasted_iota(jnp.int32, (128, 2 * ROWS), 1)
    for k in range(2):
        for h in range(2):
            hit = jnp.where(column == 2 * (f_row + h * CHUNK) + k, 1.0, 0.0)
            eb[k, h] = jnp.where(f_row < CHUNK, hit, 0.0).astype(BF16)
    npart[...] = jnp.zeros_like(npart)
    gpad[...] = jnp.zeros_like(gpad)

    d_len_local.wait()
    d_len.wait_recv()
    e_row = lax.broadcasted_iota(jnp.int32, (16, 32), 0)
    e_lane = lax.broadcasted_iota(jnp.int32, (16, 32), 1)
    e_place, e_half = lax.rem(lax.div(e_row, 2), 4), lax.rem(e_row, 2)
    wanted = mp_of(e_place, a) * 2 + e_half
    lens = jnp.where(e_row < 8, lb[0], lb[1]).astype(F32)
    len_col = jnp.sum(jnp.where(e_lane == wanted, lens, 0.0), axis=1, keepdims=True)
    slot = lax.broadcasted_iota(jnp.int32, (16, SLOT), 1).astype(F32)
    mask = jnp.where(slot < len_col, 1.0, 0.0)
    for e in range(16):
        mt[e] = mask[e : e + 1]

    def tiles(cp, i, m):
        for j in range(2):
            e = cp * 8 + i * 2 + j
            h = hb[cp, i, j, m] * mt[e].astype(BF16)
            p = jnp.dot(h, xb[cp, i, j], preferred_element_type=F32)
            p = jnp.sum((p * p).reshape(ROWS // 8, 8, D), axis=0)
            part = p[:, :128]
            for n in range(1, D // 128):
                part = part + p[:, n * 128 : (n + 1) * 128]
            npart[e] += part

    for cp in range(2):
        for s in range(2):
            w_x(cp, s, s)
            d_xf(cp, s).start()
    pl.semaphore_wait(near.at[0], 6)
    for r in range(4):
        for s in (2, 0, 1):
            for k in range(2):
                d_h(k, s, r).start()
    for to_mp in in_z:
        signal(near.at[1], dp, to_mp)

    for k in range(2):
        @pl.when(c == k)
        def _():
            for d in d_own_local(k):
                d.wait()
    own_x, own_h = xb.at[other, g], hb.at[other, :, :, a]
    remote(own_x, own_x, sxo, rxo, dp, mp).wait_recv()
    remote(own_h, own_h, sho, rho, dp, mp).wait_recv()
    loop(2, lambda cp: tiles(cp, g, a))
    for cp in range(2):
        for s in range(2):
            w_x(cp, s, 1 - s)
    loop(4, lambda n: tiles(lax.div(n, 2), mod4(g + 1 + 2 * lax.rem(n, 2)), a))
    pl.semaphore_wait(near.at[1], 2)
    for to_mp in in_z:
        signal(near.at[2], dp, to_mp)
    for cp in range(2):
        for s in range(2):
            w_xf(cp, s)
    loop(2, lambda cp: tiles(cp, mod4(g + 2), a))
    pl.semaphore_wait(near.at[2], 2)

    spot = c * 16 + mp
    r16 = lax.broadcasted_iota(jnp.int32, (16, 128), 0)
    l16 = lax.broadcasted_iota(jnp.int32, (16, 128), 1)
    far_first = sorted(
        [(dx, dz, dk) for dx in range(4) for dz in range(4) for dk in range(2) if dx or dz or dk],
        key=lambda t: -(min(t[0], 4 - t[0]) + min(t[1], 4 - t[1])),
    )

    def norm_peer(n):
        dx, dz, dk = far_first[n]
        core = c if dk == 0 else other
        return core, mod4(x + dx) * 4 + mod4(z + dz)

    def d_norm(q, n):
        core, to_mp = norm_peer(n)
        return remote(nb.at[q, spot], nb.at[q, spot], sn.at[q, n], rn.at[q, spot], y * 2 + core, to_mp)

    def norm_send(q):
        col = jnp.sum(jnp.sum(npart[...], axis=1), axis=1, keepdims=True)
        nb[q, spot] = jnp.sum(jnp.where(l16 == r16, col, 0.0), axis=0, keepdims=True)
        for n in range(31):
            d_norm(q, n).start()

    def picked(table, index, shape):
        out = jnp.zeros(shape, F32)
        for n in range(4):
            out = out + jnp.where(index == n, table[n : n + 1], 0.0)
        return out

    def factor(squares):
        return clip_limit / jnp.maximum(jnp.sqrt(squares), clip_limit)

    def norm_take(q):
        for n in range(31):
            core, from_mp = norm_peer(n)
            ref = nb.at[q, core * 16 + from_mp]
            remote(ref, ref, sn.at[q, n], rn.at[q, core * 16 + from_mp], dp, mp).wait_recv()
        rows = nb[q].reshape(32, 128)
        s0 = rows[0:4] + rows[4:8] + rows[8:12] + rows[12:16]
        s1 = jnp.concatenate(
            [jnp.sum(rows[16 + 4 * n : 20 + 4 * n], axis=0, keepdims=True) for n in range(4)], axis=0
        )
        mine = jnp.where(c == 0, s0, s1)
        others = jnp.where(c == 0, s1, s0)
        place16, half16 = lax.rem(lax.div(r16, 2), 4), lax.rem(r16, 2)
        squares = jnp.sum(
            jnp.where(l16 == r16, picked(mine, a, (16, 128)), 0.0)
            + jnp.where(l16 == lax.div(r16, 8) * 8 + a * 2 + half16, picked(others, place16, (16, 128)), 0.0),
            axis=1, keepdims=True,
        )
        scaled_mask = mask * factor(squares)
        for e in range(16):
            ft[e] = scaled_mask[e : e + 1]
        return s0, s1

    for r in range(4):
        for s in (2, 0, 1):
            for cp in range(2):
                w_h(cp, s, r)
            loop(2, lambda cp: tiles(cp, mod4(r - a), mod4(a - STEPS[s])))
        if r >= 2:
            norm_send(r - 2)
    norm_take(0)

    def owner(n):
        return mod4(a + 2 - n + 3 * (n // 2) - 2 * (n // 3))

    def products(m, ranks):
        total = None
        for r in ranks:
            for cp in range(2):
                for j in range(2):
                    i = mod4(r - a)
                    h = (hb[cp, i, j, m].astype(F32) * ft[cp * 8 + i * 2 + j]).astype(BF16)
                    p = jnp.dot(h, xb[cp, i, j], preferred_element_type=F32)
                    total = p if total is None else total + p
        return total

    def early(n):
        gall[n] = products(owner(n), (0, 1, 2))

    loop(4, early)
    s0, s1 = norm_take(1)

    def d_part(n, h):
        rows = pl.ds(h * CHUNK, CHUNK)
        return remote(gs.at[n, rows], gr.at[n, rows], sg.at[n, h], rg.at[n, h], dp, mp_of(g, owner(n)))

    for n in range(4):
        total = gall[n] + products(owner(n), (3,))
        if n < 3:
            gs[n] = total.astype(BF16)
            d_part(n, 0).start()
        else:
            gall[n] = total
        if n == 2:
            for t in range(3):
                d_part(t, 1).start()

    r32 = lax.broadcasted_iota(jnp.int32, (32, 128), 0)
    l32 = lax.broadcasted_iota(jnp.int32, (32, 128), 1)
    x32, z32, j32 = lax.div(r32, 8), lax.rem(lax.div(r32, 2), 4), lax.rem(r32, 2)
    squares = jnp.sum(
        jnp.where(l32 == c * 8 + x32 * 2 + j32, picked(s0, z32, (32, 128)), 0.0)
        + jnp.where(l32 == c * 8 + z32 * 2 + j32, picked(s1, x32, (32, 128)), 0.0),
        axis=1, keepdims=True,
    )
    clip_ref[...] = jnp.sum(
        jnp.where(l32[:, :32] == r32[:, :32], factor(squares), 0.0), axis=0, keepdims=True
    )

    def d_y(h, dy, k):
        to_dp = mod4(y + dy) * 2 + k
        return remote(ys.at[h, to_dp], yr.at[h, c, dy], sy.at[h, dy, k], ry.at[h, c, dy], to_dp, mp)

    def d_partner(h):
        to_dp = y * 2 + other
        return remote(ys.at[h, to_dp], yr.at[h, c, 0], sy.at[h, 0, 0], ry.at[h, c, 0], to_dp, mp)

    for h in range(2):
        rows = pl.ds(h * CHUNK, CHUNK)
        for n in range(3):
            ref = gr.at[n, rows]
            remote(ref, ref, sg.at[n, h], rg.at[n, h], dp, mp).wait_recv()
        gpad[0:CHUNK] = (
            gall[3, rows] + gr[0, rows].astype(F32) + gr[1, rows].astype(F32) + gr[2, rows].astype(F32)
        )
        turned = gpad[...].T.astype(BF16)
        for b in range(8):
            ys[h, b] = turned[b * OWN : (b + 1) * OWN]
        for dy in (2, 1, 3):
            for k in range(2):
                d_y(h, dy, k).start()
        d_partner(h).start()
    total = jnp.dot(ys[0, dp], eb[c, 0], preferred_element_type=F32)
    total = total + jnp.dot(ys[1, dp], eb[c, 1], preferred_element_type=F32)
    for h in range(2):
        ref = yr.at[h, other, 0]
        remote(ref, ref, sy.at[h, 0, 1], ry.at[h, other, 0], dp, mp).wait_recv()
        total = total + jnp.dot(yr[h, other, 0], eb[other, h], preferred_element_type=F32)
        for dy in (1, 3, 2):
            for k in range(2):
                ref = yr.at[h, k, dy]
                remote(ref, ref, sy.at[h, dy, k], ry.at[h, k, dy], dp, mp).wait_recv()
                total = total + jnp.dot(yr[h, k, dy], eb[k, h], preferred_element_type=F32)
    grad_ref[...] = total * (1.0 / EXAMPLES)

    d_len.wait_send()
    for k in range(2):
        @pl.when(c != k)
        def _():
            for d in d_own_remote(k):
                d.wait_send()
        for s in range(2):
            for j in range(2):
                d_x(k, s, j).wait_send()
            d_xf(k, s).wait_send()
        for s in range(3):
            for r in range(4):
                d_h(k, s, r).wait_send()
    for q in range(2):
        for n in range(31):
            d_norm(q, n).wait_send()
    for h in range(2):
        for n in range(3):
            d_part(n, h).wait_send()
        for dy in (2, 1, 3):
            for k in range(2):
                d_y(h, dy, k).wait_send()
        d_partner(h).wait_send()


def exchange(layer_input, output_cot, hidden_cot, hidden_act, lengths):
    dma = pltpu.SemaphoreType.DMA
    hbm = pl.BlockSpec(memory_space=pltpu.HBM)
    vmem = pl.BlockSpec(memory_space=pltpu.VMEM)
    return pl.pallas_call(
        kernel,
        out_shape=(jax.ShapeDtypeStruct((OWN, 2 * ROWS), F32), jax.ShapeDtypeStruct((1, 32), F32)),
        in_specs=[hbm] * 5,
        out_specs=(vmem, vmem),
        scratch_shapes=[
            pltpu.VMEM((2, 4, 2, SLOT, D), BF16),
            pltpu.VMEM((2, 4, 2, 4, ROWS, SLOT), BF16),
            pltpu.VMEM((4, ROWS, D), F32),
            pltpu.VMEM((3, ROWS, D), BF16),
            pltpu.VMEM((3, ROWS, D), BF16),
            pltpu.VMEM((128, D), F32),
            pltpu.VMEM((2, 8, OWN, 128), BF16),
            pltpu.VMEM((2, 2, 4, OWN, 128), BF16),
            pltpu.VMEM((2, 2, 128, 2 * ROWS), BF16),
            pltpu.VMEM((2, 1, 32), jnp.int32),
            pltpu.VMEM((16, 1, SLOT), F32),
            pltpu.VMEM((16, 1, SLOT), F32),
            pltpu.VMEM((16, 8, 128), F32),
            pltpu.VMEM((2, 32, 1, 128), F32),
            dma((2,)), dma, dma((2, 2, 2)), dma, dma((2, 3, 4)), dma, dma, dma((2, 2)),
            dma((2, 31)), dma((3, 2)), dma((2, 4, 2)),
            dma((2, 3, 2)), dma, dma((2, 3, 4)), dma, dma, dma((2, 32)), dma((3, 2)), dma((2, 2, 4)),
            pltpu.SemaphoreType.REGULAR((3,)),
        ],
        compiler_params=pltpu.CompilerParams(has_side_effects=True, collective_id=0, vmem_limit_bytes=60 * 1024 * 1024),
    )(layer_input, output_cot, hidden_cot, hidden_act, lengths)


def adam_kernel(grad_ref, clip_ref, w_ref, m1_ref, m2_ref, new_w_ref, new_m1_ref, new_m2_ref, out_clip_ref):
    gradient, weights = grad_ref[...], w_ref[...]
    new_moment_one = beta_one * m1_ref[...] + (1.0 - beta_one) * gradient
    new_moment_two = beta_two * m2_ref[...] + (1.0 - beta_two) * gradient * gradient
    corr_one = 1.0 - beta_one**STEP
    corr_two = 1.0 - beta_two**STEP
    direction = new_moment_one / corr_one / (jnp.sqrt(new_moment_two / corr_two) + adam_eps)
    new_w_ref[...] = weights - learn_rate * (direction + weight_decay * weights)
    new_m1_ref[...] = new_moment_one
    new_m2_ref[...] = new_moment_two
    out_clip_ref[...] = clip_ref[...]


def local(
    layer_input, output_cot, hidden_act, hidden_cot, lengths, weights, moment_one, moment_two
):
    by_place = (4, 4, 2, ROWS, SLOT)
    gradient, clip = exchange(
        layer_input, output_cot, hidden_cot.reshape(by_place), hidden_act.reshape(by_place), lengths.reshape(1, 32)
    )
    state = jax.ShapeDtypeStruct((OWN, 2 * ROWS), F32)
    new_weights, new_moment_one, new_moment_two, clip_scale = pl.pallas_call(
        adam_kernel, out_shape=(state, state, state, jax.ShapeDtypeStruct((1, 32), F32))
    )(gradient, clip, weights, moment_one, moment_two)
    return (new_weights, new_moment_one, new_moment_two, clip_scale.reshape(32))


def solution(mesh):
    return jax.shard_map(
        local,
        mesh=mesh,
        in_specs=(
            P(("dp", "mp"), None, None),
            P(("dp", "mp"), None, None),
            P("dp", "mp", None),
            P("dp", "mp", None),
            P("dp"),
            P("dp", "mp"),
            P("dp", "mp"),
            P("dp", "mp"),
        ),
        out_specs=(P("dp", "mp"), P("dp", "mp"), P("dp", "mp"), P("dp")),
        check_vma=False,
    )
```

time: 99.7 us -> 97.6 us (0.979)
  other arithmetic: 1.73 us -> 0 us
  local copies, waits for them, and re-layouts: 1.13 us -> 0 us
    pallas_call x0 -> x1, Pallas kernels: none -> 1.98 us  [local(): pl.pallas_call(adam_kernel, out_shape=(state, state, state, jax.ShapeDtyp...]
    sub x1 -> x0, other arithmetic: 1.73 us -> none  [local(): new_weights = weights - learn_rate * (direction + weight_decay * weights)]
    pallas_call x1, Pallas kernels: 96 us -> 94.8 us  [exchange(): pl.pallas_call(kernel, out_shape=(jax.ShapeDtypeStruct((OWN, 2 * ROWS), F...]
    unnamed x7 -> x0, local copies, waits for them, and re-layouts: 1.13 us -> none
where the time goes in v3:
time: 97.6 us; the launch traced here: 97.5 us
  Pallas kernels  96.8 us (99%)
    pallas_call x1, Pallas kernels, exchange(): pl.pallas_call(kernel, out_shape=(jax.ShapeDtypeStruct((OWN, 2 * ROWS), F...  94.8 us
    pallas_call x1, Pallas kernels, local(): pl.pallas_call(adam_kernel, out_shape=(state, state, state, jax.ShapeDtyp...  1.98 us

profile of v3, /device:TPU:1, one launch (start us, length us, event | category | flops | bytes accessed | tf_op | source)
XLA Modules:
  0.0 97.5 jit_solution(8248055743373302853)
XLA Ops:
  0.6 94.8 %shard_map.111 = (f32[96,384]{1,0:T(8,128)}, f32[1,32]{1,0:T(1,128)}) custom-call(bf16[2,256,768]{2,1,0:T(8,128)(2,1)} %x0_ref.1, bf16[2,256,768]{2,1,0:T(8,128)(2,1)} %x1_ref.1, bf16[4,4,2,192,256]{4,3,2,1,0:T(8,128)(2,1)} %bitcast.4, bf16[4,4,2,192,256]{4,3,2,1,0:T(8,128)(2,1)} %bitcast.5, s32[1,32]{1,0:T(1,128)} %bitcast.6), custom_call_target="tpu_custom_call" | custom-call | tf_op jit(solution)/shard_map/pallas_call | solution.py:395
  95.5 2.0 %shard_map.112 = (f32[96,384]{1,0:T(8,128)}, f32[96,384]{1,0:T(8,128)}, f32[96,384]{1,0:T(8,128)}, f32[1,32]{1,0:T(1,128)}) custom-call(f32[96,384]{1,0:T(8,128)} %get-tuple-element.10.grad_ref, f32[1,32]{1,0:T(1,128)} %get-tuple-element.11.clip_ref, f32[96,384]{1,0:T(8,128)} %w_ref.1, f32[96,384]{1,0:T(8,128)} %m1_ref.1, f32[96,384]{1,0:T(8,128)} %m2_ref.1), custom_call_target="tpu_custom_call" | custom-call | tf_op jit(solution)/shard_map/pallas_call | solution.py:445

commit v4 on v3

--- a/solution.py
+++ b/solution.py
@@ -30,9 +30,9 @@
 def kernel(
     x0_ref, x1_ref, h0_ref, h1_ref, len_ref,
     grad_ref, clip_ref,
-    xb, hb, gall, gs, gr, gpad, ys, yr, eb, lb, mt, ft, npart, nb,
-    lsem, llen, sx, sxo, sh, sho, slen, sxf, sn, sg, sy,
-    rx, rxo, rh, rho, rlen, rn, rg, ry, near,
+    xb, hb, gall, gs, gr, gh, ys, yr, yhs, yhr, hs, hr, eb, eh, lb, mt, ft, npart, nb,
+    lsem, llen, sx, sxo, sh, sho, slen, sxf, sn, sg, sy, syh, shh,
+    rx, rxo, rh, rho, rlen, rn, rg, ry, ryh, rhh, near,
 ):
     dp, mp = lax.axis_index("dp"), lax.axis_index("mp")
     c, y = lax.rem(dp, 2), lax.div(dp, 2)
@@ -57,7 +57,7 @@
 
     x_refs, h_refs = (x0_ref, x1_ref), (h0_ref, h1_ref)
     STEPS = (1, -1, 2)
-    CHUNK = ROWS // 2
+    LOW, HIGH = 128, ROWS - 128
 
     def place(k):
         return (x, z) if k == 0 else (z, x)
@@ -76,12 +76,14 @@
         return remote(x_refs[k].at[j], xb.at[c, gk, j], sx.at[k, s, j], rx.at[c, s, j],
                       y * 2 + k, mp_k(k, mod4(gk + STEPS[s]), ak))
 
-    def d_h(k, s, r):
+    def d_h(k, s, q):
         gk, ak = place(k)
         aa = mod4(ak + STEPS[s])
-        i = mod4(r - aa)
-        return remote(h_slice(k, i, aa), hb.at[c, i, :, ak], sh.at[k, s, r], rh.at[c, s, r],
-                      y * 2 + k, mp_k(k, gk, aa))
+        i = mod4(min(q, 3) - aa)
+        src, dst = h_slice(k, i, aa), hb.at[c, i, :, ak]
+        if q >= 3:
+            src, dst = src.at[q - 3], hb.at[c, i, q - 3, ak]
+        return remote(src, dst, sh.at[k, s, q], rh.at[c, s, q], y * 2 + k, mp_k(k, gk, aa))
 
     def d_own_remote(k):
         gk, ak = place(k)
@@ -112,9 +114,10 @@
         ref = xb.at[cp, mod4(g + 2), s]
         remote(ref, ref, sxf.at[0, s], rx.at[cp, 2, s], dp, mp).wait_recv()
 
-    def w_h(cp, s, r):
-        ref = hb.at[cp, mod4(r - a), :, mod4(a - STEPS[s])]
-        remote(ref, ref, sh.at[0, s, r], rh.at[cp, s, r], dp, mp).wait_recv()
+    def w_h(cp, s, q):
+        half = slice(None) if q < 3 else q - 3
+        ref = hb.at[cp, mod4(min(q, 3) - a), half, mod4(a - STEPS[s])]
+        remote(ref, ref, sh.at[0, s, q], rh.at[cp, s, q], dp, mp).wait_recv()
 
     in_x = [mod4(x + s) * 4 + z for s in STEPS[:2]]
     in_z = [x * 4 + mod4(z + s) for s in STEPS[:2]]
@@ -152,11 +155,11 @@
     f_row = lax.broadcasted_iota(jnp.int32, (128, 2 * ROWS), 0)
     column = lax.broadcasted_iota(jnp.int32, (128, 2 * ROWS), 1)
     for k in range(2):
-        for h in range(2):
-            hit = jnp.where(column == 2 * (f_row + h * CHUNK) + k, 1.0, 0.0)
-            eb[k, h] = jnp.where(f_row < CHUNK, hit, 0.0).astype(BF16)
+        eb[k] = jnp.where(column == 2 * f_row + k, 1.0, 0.0).astype(BF16)
+        high = f_row - HIGH * lax.rem(place(k)[1], 2)
+        hit = jnp.where(column == 2 * (LOW + high) + k, 1.0, 0.0)
+        eh[k] = jnp.where(high < HIGH, jnp.where(high >= 0, hit, 0.0), 0.0).astype(BF16)
     npart[...] = jnp.zeros_like(npart)
-    gpad[...] = jnp.zeros_like(gpad)
 
     d_len_local.wait()
     d_len.wait_recv()
@@ -171,8 +174,8 @@
     for e in range(16):
         mt[e] = mask[e : e + 1]
 
-    def tiles(cp, i, m):
-        for j in range(2):
+    def tiles(cp, i, m, halves=(0, 1)):
+        for j in halves:
             e = cp * 8 + i * 2 + j
             h = hb[cp, i, j, m] * mt[e].astype(BF16)
             p = jnp.dot(h, xb[cp, i, j], preferred_element_type=F32)
@@ -187,10 +190,10 @@
             w_x(cp, s, s)
             d_xf(cp, s).start()
     pl.semaphore_wait(near.at[0], 6)
-    for r in range(4):
+    for q in range(5):
         for s in (2, 0, 1):
             for k in range(2):
-                d_h(k, s, r).start()
+                d_h(k, s, q).start()
     for to_mp in in_z:
         signal(near.at[1], dp, to_mp)
 
@@ -271,13 +274,18 @@
             ft[e] = scaled_mask[e : e + 1]
         return s0, s1
 
-    for r in range(4):
+    for q in range(5):
         for s in (2, 0, 1):
             for cp in range(2):
-                w_h(cp, s, r)
-            loop(2, lambda cp: tiles(cp, mod4(r - a), mod4(a - STEPS[s])))
-        if r >= 2:
-            norm_send(r - 2)
+                w_h(cp, s, q)
+            if q < 3:
+                loop(2, lambda cp: tiles(cp, mod4(q - a), mod4(a - STEPS[s])))
+            else:
+                for cp in range(2):
+                    tiles(cp, mod4(3 - a), mod4(a - STEPS[s]), (q - 3,))
+        if q == 2:
+            norm_send(0)
+    norm_send(1)
     norm_take(0)
 
     def owner(n):
@@ -300,20 +308,47 @@
     loop(4, early)
     s0, s1 = norm_take(1)
 
-    def d_part(n, h):
-        rows = pl.ds(h * CHUNK, CHUNK)
-        return remote(gs.at[n, rows], gr.at[n, rows], sg.at[n, h], rg.at[n, h], dp, mp_of(g, owner(n)))
+    def d_part(n):
+        return remote(gs.at[n], gr.at[n], sg.at[n], rg.at[n], dp, mp_of(g, owner(n)))
 
     for n in range(4):
-        total = gall[n] + products(owner(n), (3,))
+        m = owner(n)
+        total = gall[n] + products(m, (3,))
+        gh[pl.ds(pl.multiple_of(m * HIGH, HIGH), HIGH)] = total[LOW:]
         if n < 3:
-            gs[n] = total.astype(BF16)
-            d_part(n, 0).start()
+            gs[n] = total[:LOW].astype(BF16)
+            d_part(n).start()
         else:
-            gall[n] = total
-        if n == 2:
-            for t in range(3):
-                d_part(t, 1).start()
+            gall[n, :LOW] = total[:LOW]
+
+    def d_y(src, dst, ssem, rsem, dy, k):
+        to_dp = mod4(y + dy) * 2 + k
+        return remote(src.at[to_dp], dst.at[c, dy], ssem.at[dy, k], rsem.at[c, dy], to_dp, mp)
+
+    def d_partner(src, dst, ssem, rsem):
+        to_dp = y * 2 + other
+        return remote(src.at[to_dp], dst.at[c, 0], ssem.at[0, 0], rsem.at[c, 0], to_dp, mp)
+
+    def y_start(*refs):
+        for dy in (2, 1, 3):
+            for k in range(2):
+                d_y(*refs, dy, k).start()
+        d_partner(*refs).start()
+
+    def y_wait(src, dst, ssem, rsem):
+        ref = dst.at[other, 0]
+        remote(ref, ref, ssem.at[0, 1], rsem.at[other, 0], dp, mp).wait_recv()
+        for dy in (1, 3, 2):
+            for k in range(2):
+                ref = dst.at[k, dy]
+                remote(ref, ref, ssem.at[dy, k], rsem.at[k, dy], dp, mp).wait_recv()
+
+    over_low, over_high = (ys, yr, sy, ry), (yhs, yhr, syh, ryh)
+    turned = gh[...].T.astype(BF16)
+    for b in range(8):
+        yhs[b] = turned[b * OWN : (b + 1) * OWN]
+    y_start(*over_high)
+    yhr[c, 0] = yhs[dp]
 
     r32 = lax.broadcasted_iota(jnp.int32, (32, 128), 0)
     l32 = lax.broadcasted_iota(jnp.int32, (32, 128), 1)
@@ -327,40 +362,39 @@
         jnp.where(l32[:, :32] == r32[:, :32], factor(squares), 0.0), axis=0, keepdims=True
     )
 
-    def d_y(h, dy, k):
-        to_dp = mod4(y + dy) * 2 + k
-        return remote(ys.at[h, to_dp], yr.at[h, c, dy], sy.at[h, dy, k], ry.at[h, c, dy], to_dp, mp)
-
-    def d_partner(h):
-        to_dp = y * 2 + other
-        return remote(ys.at[h, to_dp], yr.at[h, c, 0], sy.at[h, 0, 0], ry.at[h, c, 0], to_dp, mp)
-
-    for h in range(2):
-        rows = pl.ds(h * CHUNK, CHUNK)
-        for n in range(3):
-            ref = gr.at[n, rows]
-            remote(ref, ref, sg.at[n, h], rg.at[n, h], dp, mp).wait_recv()
-        gpad[0:CHUNK] = (
-            gall[3, rows] + gr[0, rows].astype(F32) + gr[1, rows].astype(F32) + gr[2, rows].astype(F32)
-        )
-        turned = gpad[...].T.astype(BF16)
-        for b in range(8):
-            ys[h, b] = turned[b * OWN : (b + 1) * OWN]
-        for dy in (2, 1, 3):
-            for k in range(2):
-                d_y(h, dy, k).start()
-        d_partner(h).start()
-    total = jnp.dot(ys[0, dp], eb[c, 0], preferred_element_type=F32)
-    total = total + jnp.dot(ys[1, dp], eb[c, 1], preferred_element_type=F32)
-    for h in range(2):
-        ref = yr.at[h, other, 0]
-        remote(ref, ref, sy.at[h, 0, 1], ry.at[h, other, 0], dp, mp).wait_recv()
-        total = total + jnp.dot(yr[h, other, 0], eb[other, h], preferred_element_type=F32)
-        for dy in (1, 3, 2):
-            for k in range(2):
-                ref = yr.at[h, k, dy]
-                remote(ref, ref, sy.at[h, dy, k], ry.at[h, k, dy], dp, mp).wait_recv()
-                total = total + jnp.dot(yr[h, k, dy], eb[k, h], preferred_element_type=F32)
+    for n in range(3):
+        remote(gr.at[n], gr.at[n], sg.at[n], rg.at[n], dp, mp).wait_recv()
+    low = gall[3, :LOW] + gr[0].astype(F32) + gr[1].astype(F32) + gr[2].astype(F32)
+    turned = low.T.astype(BF16)
+    for b in range(8):
+        ys[b] = turned[b * OWN : (b + 1) * OWN]
+    y_start(*over_low)
+    yr[c, 0] = ys[dp]
+
+    def d_high(k, s):
+        gk, ak = place(k)
+        aa = mod4(ak + STEPS[s])
+        return remote(hs.at[k, lax.div(aa, 2)], hr.at[k, s], shh.at[k, s], rhh.at[k, s], dp, mp_k(k, gk, aa))
+
+    y_wait(*over_high)
+    for k in range(2):
+        high = yhr[k, 0].astype(F32)
+        for dy in range(1, 4):
+            high = high + yhr[k, dy].astype(F32)
+        for t in range(2):
+            hs[k, t] = high[:, t * 128 : (t + 1) * 128].astype(BF16)
+        for s in (2, 0, 1):
+            d_high(k, s).start()
+    total = jnp.dot(hs[0, lax.div(place(0)[1], 2)], eh[0], preferred_element_type=F32)
+    total = total + jnp.dot(hs[1, lax.div(place(1)[1], 2)], eh[1], preferred_element_type=F32)
+    y_wait(*over_low)
+    for k in range(2):
+        for dy in range(4):
+            total = total + jnp.dot(yr[k, dy], eb[k], preferred_element_type=F32)
+    for k in range(2):
+        for s in (0, 1, 2):
+            remote(hr.at[k, s], hr.at[k, s], shh.at[k, s], rhh.at[k, s], dp, mp).wait_recv()
+            total = total + jnp.dot(hr[k, s], eh[k], preferred_element_type=F32)
     grad_ref[...] = total * (1.0 / EXAMPLES)
 
     d_len.wait_send()
@@ -374,18 +408,19 @@
                 d_x(k, s, j).wait_send()
             d_xf(k, s).wait_send()
         for s in range(3):
-            for r in range(4):
-                d_h(k, s, r).wait_send()
+            for q in range(5):
+                d_h(k, s, q).wait_send()
+            d_high(k, s).wait_send()
     for q in range(2):
         for n in range(31):
             d_norm(q, n).wait_send()
-    for h in range(2):
-        for n in range(3):
-            d_part(n, h).wait_send()
+    for n in range(3):
+        d_part(n).wait_send()
+    for refs in (over_low, over_high):
         for dy in (2, 1, 3):
             for k in range(2):
-                d_y(h, dy, k).wait_send()
-        d_partner(h).wait_send()
+                d_y(*refs, dy, k).wait_send()
+        d_partner(*refs).wait_send()
 
 
 def exchange(layer_input, output_cot, hidden_cot, hidden_act, lengths):
@@ -401,37 +436,29 @@
             pltpu.VMEM((2, 4, 2, SLOT, D), BF16),
             pltpu.VMEM((2, 4, 2, 4, ROWS, SLOT), BF16),
             pltpu.VMEM((4, ROWS, D), F32),
-            pltpu.VMEM((3, ROWS, D), BF16),
-            pltpu.VMEM((3, ROWS, D), BF16),
-            pltpu.VMEM((128, D), F32),
-            pltpu.VMEM((2, 8, OWN, 128), BF16),
-            pltpu.VMEM((2, 2, 4, OWN, 128), BF16),
-            pltpu.VMEM((2, 2, 128, 2 * ROWS), BF16),
+            pltpu.VMEM((3, 128, D), BF16),
+            pltpu.VMEM((3, 128, D), BF16),
+            pltpu.VMEM((256, D), F32),
+            pltpu.VMEM((8, OWN, 128), BF16),
+            pltpu.VMEM((2, 4, OWN, 128), BF16),
+            pltpu.VMEM((8, OWN, 256), BF16),
+            pltpu.VMEM((2, 4, OWN, 256), BF16),
+            pltpu.VMEM((2, 2, OWN, 128), BF16),
+            pltpu.VMEM((2, 3, OWN, 128), BF16),
+            pltpu.VMEM((2, 128, 2 * ROWS), BF16),
+            pltpu.VMEM((2, 128, 2 * ROWS), BF16),
             pltpu.VMEM((2, 1, 32), jnp.int32),
             pltpu.VMEM((16, 1, SLOT), F32),
             pltpu.VMEM((16, 1, SLOT), F32),
             pltpu.VMEM((16, 8, 128), F32),
             pltpu.VMEM((2, 32, 1, 128), F32),
-            dma((2,)), dma, dma((2, 2, 2)), dma, dma((2, 3, 4)), dma, dma, dma((2, 2)),
-            dma((2, 31)), dma((3, 2)), dma((2, 4, 2)),
-            dma((2, 3, 2)), dma, dma((2, 3, 4)), dma, dma, dma((2, 32)), dma((3, 2)), dma((2, 2, 4)),
+            dma((2,)), dma, dma((2, 2, 2)), dma, dma((2, 3, 5)), dma, dma, dma((2, 2)),
+            dma((2, 31)), dma((3,)), dma((4, 2)), dma((4, 2)), dma((2, 3)),
+            dma((2, 3, 2)), dma, dma((2, 3, 5)), dma, dma, dma((2, 32)), dma((3,)), dma((2, 4)), dma((2, 4)), dma((2, 3)),
             pltpu.SemaphoreType.REGULAR((3,)),
         ],
-        compiler_params=pltpu.CompilerParams(has_side_effects=True, collective_id=0, vmem_limit_bytes=60 * 1024 * 1024),
+        compiler_params=pltpu.CompilerParams(has_side_effects=True, collective_id=0, vmem_limit_bytes=56_000_000),
     )(layer_input, output_cot, hidden_cot, hidden_act, lengths)
-
-
-def adam_kernel(grad_ref, clip_ref, w_ref, m1_ref, m2_ref, new_w_ref, new_m1_ref, new_m2_ref, out_clip_ref):
-    gradient, weights = grad_ref[...], w_ref[...]
-    new_moment_one = beta_one * m1_ref[...] + (1.0 - beta_one) * gradient
-    new_moment_two = beta_two * m2_ref[...] + (1.0 - beta_two) * gradient * gradient
-    corr_one = 1.0 - beta_one**STEP
-    corr_two = 1.0 - beta_two**STEP
-    direction = new_moment_one / corr_one / (jnp.sqrt(new_moment_two / corr_two) + adam_eps)
-    new_w_ref[...] = weights - learn_rate * (direction + weight_decay * weights)
-    new_m1_ref[...] = new_moment_one
-    new_m2_ref[...] = new_moment_two
-    out_clip_ref[...] = clip_ref[...]
 
 
 def local(
@@ -441,11 +468,13 @@
     gradient, clip = exchange(
         layer_input, output_cot, hidden_cot.reshape(by_place), hidden_act.reshape(by_place), lengths.reshape(1, 32)
     )
-    state = jax.ShapeDtypeStruct((OWN, 2 * ROWS), F32)
-    new_weights, new_moment_one, new_moment_two, clip_scale = pl.pallas_call(
-        adam_kernel, out_shape=(state, state, state, jax.ShapeDtypeStruct((1, 32), F32))
-    )(gradient, clip, weights, moment_one, moment_two)
-    return (new_weights, new_moment_one, new_moment_two, clip_scale.reshape(32))
+    new_moment_one = beta_one * moment_one + (1.0 - beta_one) * gradient
+    new_moment_two = beta_two * moment_two + (1.0 - beta_two) * gradient * gradient
+    corr_one = 1.0 - beta_one**STEP
+    corr_two = 1.0 - beta_two**STEP
+    direction = new_moment_one / corr_one / (jnp.sqrt(new_moment_two / corr_two) + adam_eps)
+    new_weights = weights - learn_rate * (direction + weight_decay * weights)
+    return (new_weights, new_moment_one, new_moment_two, clip.reshape(32))
 
 
 def solution(mesh):

time: 97.6 us -> 94.6 us (0.969)
  Pallas kernels: 96.8 us -> 91.8 us
  local copies, waits for them, and re-layouts: 0 us -> 1.17 us
    pallas_call x1, Pallas kernels: 94.8 us -> 91.8 us  [exchange(): pl.pallas_call(kernel, out_shape=(jax.ShapeDtypeStruct((OWN, 2 * ROWS), F...]
    pallas_call x1 -> x0, Pallas kernels: 1.98 us -> none  [local(): pl.pallas_call(adam_kernel, out_shape=(state, state, state, jax.ShapeDtyp...]
    unnamed x0 -> x9, local copies, waits for them, and re-layouts: none -> 1.17 us
where the time goes in v4:
time: 94.6 us; the launch traced here: 94.5 us
  Pallas kernels  91.8 us (97%)
  local copies, waits for them, and re-layouts  1.17 us (1%)
    pallas_call x1, Pallas kernels, exchange(): pl.pallas_call(kernel, out_shape=(jax.ShapeDtypeStruct((OWN, 2 * ROWS), F...  91.8 us

profile of v4, /device:TPU:1, one launch (start us, length us, event | category | flops | bytes accessed | tf_op | source)
XLA Modules:
  0.0 94.5 jit_solution(10736332986006429655)
XLA Ops:
  0.6 0.0 copy-start
  0.6 0.6 copy-done
  1.3 0.0 copy-start.1
  1.3 0.0 copy-start.2
  1.3 0.0 copy-start.3
  1.3 91.8 %shard_map.111 = (f32[96,384]{1,0:T(8,128)S(1)}, f32[1,32]{1,0:T(1,128)S(1)}) custom-call(bf16[2,256,768]{2,1,0:T(8,128)(2,1)} %x0_ref.1, bf16[2,256,768]{2,1,0:T(8,128)(2,1)} %x1_ref.1, bf16[4,4,2,192,256]{4,3,2,1,0:T(8,128)(2,1)} %bitcast.6, bf16[4,4,2,192,256]{4,3,2,1,0:T(8,128)(2,1)} %bitcast.7, s32[1,32]{1,0:T(1,128)S(1)} %bitcast.4), custom_call_target="tpu_custom_call" | custom-call | tf_op jit(solution)/shard_map/pallas_call | solution.py:430
  93.1 0.0 copy-done.1
  93.1 0.0 copy-done.2
  93.2 0.0 copy-done.3
  93.2 0.8 multiply_subtract_fusion
  94.0 0.5 copy.13
Async XLA Ops:
  0.6 0.7 copy-start
  1.3 91.8 %copy-start.1 = (f32[96,384]{1,0:T(8,128)S(1)}, f32[96,384]{1,0:T(8,128)}, u32[]{:S(2)}) copy-start(f32[96,384]{1,0:T(8,128)} %param.13) | copy-start | bytes 442372
  1.3 91.9 %copy-start.2 = (f32[96,384]{1,0:T(8,128)S(1)}, f32[96,384]{1,0:T(8,128)}, u32[]{:S(2)}) copy-start(f32[96,384]{1,0:T(8,128)} %param.14) | copy-start | bytes 442372
  1.3 91.9 %copy-start.3 = (f32[96,384]{1,0:T(8,128)S(1)}, f32[96,384]{1,0:T(8,128)}, u32[]{:S(2)}) copy-start(f32[96,384]{1,0:T(8,128)} %param.15) | copy-start | bytes 442372

commit v5 on v4

--- a/solution.py
+++ b/solution.py
@@ -30,7 +30,7 @@
 def kernel(
     x0_ref, x1_ref, h0_ref, h1_ref, len_ref,
     grad_ref, clip_ref,
-    xb, hb, gall, gs, gr, gh, ys, yr, yhs, yhr, hs, hr, eb, eh, lb, mt, ft, npart, nb,
+    xb, hb, gall, gs, gr, gh, ys, yr, yhs, yhr, hs, hr, eb, eh, lb, mt, ft, fc, npart, nb, p3,
     lsem, llen, sx, sxo, sh, sho, slen, sxf, sn, sg, sy, syh, shh,
     rx, rxo, rh, rho, rlen, rn, rg, ry, ryh, rhh, near,
 ):
@@ -174,11 +174,16 @@
     for e in range(16):
         mt[e] = mask[e : e + 1]
 
-    def tiles(cp, i, m, halves=(0, 1)):
+    def masked_product(cp, i, j, m):
+        h = hb[cp, i, j, m] * mt[cp * 8 + i * 2 + j].astype(BF16)
+        return jnp.dot(h, xb[cp, i, j], preferred_element_type=F32)
+
+    def tiles(cp, i, m, halves=(0, 1), keep=False):
         for j in halves:
             e = cp * 8 + i * 2 + j
-            h = hb[cp, i, j, m] * mt[e].astype(BF16)
-            p = jnp.dot(h, xb[cp, i, j], preferred_element_type=F32)
+            p = masked_product(cp, i, j, m)
+            if keep:
+                p3[cp, j, m] = p
             p = jnp.sum((p * p).reshape(ROWS // 8, 8, D), axis=0)
             part = p[:, :128]
             for n in range(1, D // 128):
@@ -190,10 +195,13 @@
             w_x(cp, s, s)
             d_xf(cp, s).start()
     pl.semaphore_wait(near.at[0], 6)
-    for q in range(5):
-        for s in (2, 0, 1):
-            for k in range(2):
-                d_h(k, s, q).start()
+    def send_rank(*parts):
+        for q in parts:
+            for s in (2, 0, 1):
+                for k in range(2):
+                    d_h(k, s, q).start()
+
+    send_rank(0, 1, 2)
     for to_mp in in_z:
         signal(near.at[1], dp, to_mp)
 
@@ -217,6 +225,9 @@
         for s in range(2):
             w_xf(cp, s)
     loop(2, lambda cp: tiles(cp, mod4(g + 2), a))
+    for cp in range(2):
+        for j in range(2):
+            p3[cp, j, a] = masked_product(cp, mod4(3 - a), j, a)
     pl.semaphore_wait(near.at[2], 2)
 
     spot = c * 16 + mp
@@ -269,24 +280,15 @@
             + jnp.where(l16 == lax.div(r16, 8) * 8 + a * 2 + half16, picked(others, place16, (16, 128)), 0.0),
             axis=1, keepdims=True,
         )
-        scaled_mask = mask * factor(squares)
-        for e in range(16):
-            ft[e] = scaled_mask[e : e + 1]
+        scale = factor(squares)
+        if q == 2:
+            for e in range(16):
+                fc[e] = jnp.broadcast_to(scale[e : e + 1], (1, D))
+        else:
+            scaled_mask = mask * scale
+            for e in range(16):
+                ft[e] = scaled_mask[e : e + 1]
         return s0, s1
-
-    for q in range(5):
-        for s in (2, 0, 1):
-            for cp in range(2):
-                w_h(cp, s, q)
-            if q < 3:
-                loop(2, lambda cp: tiles(cp, mod4(q - a), mod4(a - STEPS[s])))
-            else:
-                for cp in range(2):
-                    tiles(cp, mod4(3 - a), mod4(a - STEPS[s]), (q - 3,))
-        if q == 2:
-            norm_send(0)
-    norm_send(1)
-    norm_take(0)
 
     def owner(n):
         return mod4(a + 2 - n + 3 * (n // 2) - 2 * (n // 3))
@@ -303,23 +305,53 @@
         return total
 
     def early(n):
-        gall[n] = products(owner(n), (0, 1, 2))
-
-    loop(4, early)
-    s0, s1 = norm_take(1)
+        gall[n] = products(owner(n), (0, 1))
+
+    def third(n):
+        gall[n] += products(owner(n), (2,))
+
+    for q in range(5):
+        for s in (2, 0, 1):
+            for cp in range(2):
+                w_h(cp, s, q)
+            if q < 3:
+                loop(2, lambda cp: tiles(cp, mod4(q - a), mod4(a - STEPS[s])))
+            else:
+                for cp in range(2):
+                    tiles(cp, mod4(3 - a), mod4(a - STEPS[s]), (q - 3,), True)
+        if q in (1, 2):
+            norm_send(q - 1)
+        if q == 1:
+            send_rank(3, 4)
+        if q == 2:
+            norm_take(0)
+            loop(4, early)
+    norm_send(2)
+    norm_take(1)
+    loop(4, third)
+    s0, s1 = norm_take(2)
 
     def d_part(n):
         return remote(gs.at[n], gr.at[n], sg.at[n], rg.at[n], dp, mp_of(g, owner(n)))
 
+    def final_rows(n, row):
+        rows = pl.ds(row, 16)
+        total = gall[n, rows]
+        for cp in range(2):
+            for j in range(2):
+                total = total + fc[cp * 8 + mod4(3 - a) * 2 + j] * p3[cp, j, owner(n), rows]
+        return total
+
     for n in range(4):
-        m = owner(n)
-        total = gall[n] + products(m, (3,))
-        gh[pl.ds(pl.multiple_of(m * HIGH, HIGH), HIGH)] = total[LOW:]
+        for row in range(0, LOW, 16):
+            if n < 3:
+                gs[n, row : row + 16] = final_rows(n, row).astype(BF16)
+            else:
+                gall[n, row : row + 16] = final_rows(n, row)
         if n < 3:
-            gs[n] = total[:LOW].astype(BF16)
             d_part(n).start()
-        else:
-            gall[n, :LOW] = total[:LOW]
+        for row in range(LOW, ROWS, 16):
+            gh[pl.ds(pl.multiple_of(owner(n) * HIGH + row - LOW, 16), 16)] = final_rows(n, row)
 
     def d_y(src, dst, ssem, rsem, dy, k):
         to_dp = mod4(y + dy) * 2 + k
@@ -411,7 +443,7 @@
             for q in range(5):
                 d_h(k, s, q).wait_send()
             d_high(k, s).wait_send()
-    for q in range(2):
+    for q in range(3):
         for n in range(31):
             d_norm(q, n).wait_send()
     for n in range(3):
@@ -450,11 +482,13 @@
             pltpu.VMEM((2, 1, 32), jnp.int32),
             pltpu.VMEM((16, 1, SLOT), F32),
             pltpu.VMEM((16, 1, SLOT), F32),
+            pltpu.VMEM((16, 1, D), F32),
             pltpu.VMEM((16, 8, 128), F32),
-            pltpu.VMEM((2, 32, 1, 128), F32),
+            pltpu.VMEM((3, 32, 1, 128), F32),
+            pltpu.VMEM((2, 2, 4, ROWS, D), F32),
             dma((2,)), dma, dma((2, 2, 2)), dma, dma((2, 3, 5)), dma, dma, dma((2, 2)),
-            dma((2, 31)), dma((3,)), dma((4, 2)), dma((4, 2)), dma((2, 3)),
-            dma((2, 3, 2)), dma, dma((2, 3, 5)), dma, dma, dma((2, 32)), dma((3,)), dma((2, 4)), dma((2, 4)), dma((2, 3)),
+            dma((3, 31)), dma((3,)), dma((4, 2)), dma((4, 2)), dma((2, 3)),
+            dma((2, 3, 2)), dma, dma((2, 3, 5)), dma, dma, dma((3, 32)), dma((3,)), dma((2, 4)), dma((2, 4)), dma((2, 3)),
             pltpu.SemaphoreType.REGULAR((3,)),
         ],
         compiler_params=pltpu.CompilerParams(has_side_effects=True, collective_id=0, vmem_limit_bytes=56_000_000),

time: 94.6 us -> 93.7 us (level)
  no operation moved by 1% of the time
where the time goes in v5:
time: 93.7 us; the launch traced here: 93.6 us
  Pallas kernels  90.9 us (97%)
  local copies, waits for them, and re-layouts  1.17 us (1%)
    pallas_call x1, Pallas kernels, exchange(): pl.pallas_call(kernel, out_shape=(jax.ShapeDtypeStruct((OWN, 2 * ROWS), F...  90.9 us

profile of v5, /device:TPU:1, one launch (start us, length us, event | category | flops | bytes accessed | tf_op | source)
XLA Modules:
  0.0 93.6 jit_solution(8406407845018545060)
XLA Ops:
  0.6 0.0 copy-start
  0.6 0.6 copy-done
  1.3 0.0 copy-start.1
  1.3 0.0 copy-start.2
  1.3 0.0 copy-start.3
  1.3 90.9 %shard_map.111 = (f32[96,384]{1,0:T(8,128)S(1)}, f32[1,32]{1,0:T(1,128)S(1)}) custom-call(bf16[2,256,768]{2,1,0:T(8,128)(2,1)} %x0_ref.1, bf16[2,256,768]{2,1,0:T(8,128)(2,1)} %x1_ref.1, bf16[4,4,2,192,256]{4,3,2,1,0:T(8,128)(2,1)} %bitcast.6, bf16[4,4,2,192,256]{4,3,2,1,0:T(8,128)(2,1)} %bitcast.7, s32[1,32]{1,0:T(1,128)S(1)} %bitcast.4), custom_call_target="tpu_custom_call" | custom-call | tf_op jit(solution)/shard_map/pallas_call | solution.py:462
  92.2 0.0 copy-done.1
  92.3 0.0 copy-done.2
  92.3 0.0 copy-done.3
  92.3 0.8 multiply_subtract_fusion
  93.1 0.5 copy.13
Async XLA Ops:
  0.6 0.7 copy-start
  1.3 91.0 %copy-start.1 = (f32[96,384]{1,0:T(8,128)S(1)}, f32[96,384]{1,0:T(8,128)}, u32[]{:S(2)}) copy-start(f32[96,384]{1,0:T(8,128)} %param.13) | copy-start | bytes 442372
  1.3 91.0 %copy-start.2 = (f32[96,384]{1,0:T(8,128)S(1)}, f32[96,384]{1,0:T(8,128)}, u32[]{:S(2)}) copy-start(f32[96,384]{1,0:T(8,128)} %param.14) | copy-start | bytes 442372
  1.3 91.0 %copy-start.3 = (f32[96,384]{1,0:T(8,128)S(1)}, f32[96,384]{1,0:T(8,128)}, u32[]{:S(2)}) copy-start(f32[96,384]{1,0:T(8,128)} %param.15) | copy-start | bytes 442372

commit v6 on v5

--- a/solution.py
+++ b/solution.py
@@ -234,14 +234,18 @@
     r16 = lax.broadcasted_iota(jnp.int32, (16, 128), 0)
     l16 = lax.broadcasted_iota(jnp.int32, (16, 128), 1)
     far_first = sorted(
-        [(dx, dz, dk) for dx in range(4) for dz in range(4) for dk in range(2) if dx or dz or dk],
+        [(dx, dz) for dx in range(4) for dz in range(4)],
         key=lambda t: -(min(t[0], 4 - t[0]) + min(t[1], 4 - t[1])),
     )
+    same_core = [(2, 0), (1, 0), (3, 0)] + [(dg, da) for da in (2, 1, 3) for dg in range(4)]
+    NEEDED, ALL = 19, 31
 
     def norm_peer(n):
-        dx, dz, dk = far_first[n]
-        core = c if dk == 0 else other
-        return core, mod4(x + dx) * 4 + mod4(z + dz)
+        if n < 16:
+            dx, dz = far_first[n]
+            return other, mod4(x + dx) * 4 + mod4(z + dz)
+        dg, da = same_core[n - 16]
+        return c, mp_of(mod4(g + dg), mod4(a + da))
 
     def d_norm(q, n):
         core, to_mp = norm_peer(n)
@@ -250,7 +254,7 @@
     def norm_send(q):
         col = jnp.sum(jnp.sum(npart[...], axis=1), axis=1, keepdims=True)
         nb[q, spot] = jnp.sum(jnp.where(l16 == r16, col, 0.0), axis=0, keepdims=True)
-        for n in range(31):
+        for n in range(NEEDED):
             d_norm(q, n).start()
 
     def picked(table, index, shape):
@@ -262,21 +266,30 @@
     def factor(squares):
         return clip_limit / jnp.maximum(jnp.sqrt(squares), clip_limit)
 
-    def norm_take(q):
-        for n in range(31):
+    def norm_wait(q, first, last):
+        for n in range(first, last):
             core, from_mp = norm_peer(n)
             ref = nb.at[q, core * 16 + from_mp]
             remote(ref, ref, sn.at[q, n], rn.at[q, core * 16 + from_mp], dp, mp).wait_recv()
-        rows = nb[q].reshape(32, 128)
-        s0 = rows[0:4] + rows[4:8] + rows[8:12] + rows[12:16]
-        s1 = jnp.concatenate(
-            [jnp.sum(rows[16 + 4 * n : 20 + 4 * n], axis=0, keepdims=True) for n in range(4)], axis=0
+
+    def over_x(rows):
+        return rows[0:4] + rows[4:8] + rows[8:12] + rows[12:16]
+
+    def over_z(rows):
+        return jnp.concatenate(
+            [jnp.sum(rows[4 * n : 4 * n + 4], axis=0, keepdims=True) for n in range(4)], axis=0
         )
-        mine = jnp.where(c == 0, s0, s1)
-        others = jnp.where(c == 0, s1, s0)
+
+    def norm_take(q):
+        norm_wait(q, 0, NEEDED)
+        rows = nb[q, pl.ds(other * 16, 16)].reshape(16, 128)
+        others = jnp.where(c == 0, over_z(rows), over_x(rows))
+        mine = nb[q, c * 16 + mp_of(0, a)]
+        for n in range(1, 4):
+            mine = mine + nb[q, c * 16 + mp_of(n, a)]
         place16, half16 = lax.rem(lax.div(r16, 2), 4), lax.rem(r16, 2)
         squares = jnp.sum(
-            jnp.where(l16 == r16, picked(mine, a, (16, 128)), 0.0)
+            jnp.where(l16 == r16, mine, 0.0)
             + jnp.where(l16 == lax.div(r16, 8) * 8 + a * 2 + half16, picked(others, place16, (16, 128)), 0.0),
             axis=1, keepdims=True,
         )
@@ -288,7 +301,6 @@
             scaled_mask = mask * scale
             for e in range(16):
                 ft[e] = scaled_mask[e : e + 1]
-        return s0, s1
 
     def owner(n):
         return mod4(a + 2 - n + 3 * (n // 2) - 2 * (n // 3))
@@ -329,7 +341,7 @@
     norm_send(2)
     norm_take(1)
     loop(4, third)
-    s0, s1 = norm_take(2)
+    norm_take(2)
 
     def d_part(n):
         return remote(gs.at[n], gr.at[n], sg.at[n], rg.at[n], dp, mp_of(g, owner(n)))
@@ -376,12 +388,26 @@
                 remote(ref, ref, ssem.at[dy, k], rsem.at[k, dy], dp, mp).wait_recv()
 
     over_low, over_high = (ys, yr, sy, ry), (yhs, yhr, syh, ryh)
+    for n in range(NEEDED, ALL):
+        d_norm(2, n).start()
     turned = gh[...].T.astype(BF16)
     for b in range(8):
         yhs[b] = turned[b * OWN : (b + 1) * OWN]
     y_start(*over_high)
     yhr[c, 0] = yhs[dp]
 
+    for n in range(3):
+        remote(gr.at[n], gr.at[n], sg.at[n], rg.at[n], dp, mp).wait_recv()
+    low = gall[3, :LOW] + gr[0].astype(F32) + gr[1].astype(F32) + gr[2].astype(F32)
+    turned = low.T.astype(BF16)
+    for b in range(8):
+        ys[b] = turned[b * OWN : (b + 1) * OWN]
+    y_start(*over_low)
+    yr[c, 0] = ys[dp]
+
+    norm_wait(2, NEEDED, ALL)
+    rows = nb[2].reshape(32, 128)
+    s0, s1 = over_x(rows[:16]), over_z(rows[16:])
     r32 = lax.broadcasted_iota(jnp.int32, (32, 128), 0)
     l32 = lax.broadcasted_iota(jnp.int32, (32, 128), 1)
     x32, z32, j32 = lax.div(r32, 8), lax.rem(lax.div(r32, 2), 4), lax.rem(r32, 2)
@@ -393,15 +419,6 @@
     clip_ref[...] = jnp.sum(
         jnp.where(l32[:, :32] == r32[:, :32], factor(squares), 0.0), axis=0, keepdims=True
     )
-
-    for n in range(3):
-        remote(gr.at[n], gr.at[n], sg.at[n], rg.at[n], dp, mp).wait_recv()
-    low = gall[3, :LOW] + gr[0].astype(F32) + gr[1].astype(F32) + gr[2].astype(F32)
-    turned = low.T.astype(BF16)
-    for b in range(8):
-        ys[b] = turned[b * OWN : (b + 1) * OWN]
-    y_start(*over_low)
-    yr[c, 0] = ys[dp]
 
     def d_high(k, s):
         gk, ak = place(k)
@@ -444,7 +461,7 @@
                 d_h(k, s, q).wait_send()
             d_high(k, s).wait_send()
     for q in range(3):
-        for n in range(31):
+        for n in range(NEEDED if q < 2 else ALL):
             d_norm(q, n).wait_send()
     for n in range(3):
         d_part(n).wait_send()

time: 93.7 us -> 93.1 us (level)
  no operation moved by 1% of the time
where the time goes in v6:
time: 93.1 us; the launch traced here: 93 us
  Pallas kernels  90.4 us (97%)
  local copies, waits for them, and re-layouts  1.17 us (1%)
    pallas_call x1, Pallas kernels, exchange(): pl.pallas_call(kernel, out_shape=(jax.ShapeDtypeStruct((OWN, 2 * ROWS), F...  90.4 us

profile of v6, /device:TPU:1, one launch (start us, length us, event | category | flops | bytes accessed | tf_op | source)
XLA Modules:
  0.0 93.0 jit_solution(7729540967152198480)
XLA Ops:
  0.6 0.0 copy-start
  0.6 0.6 copy-done
  1.3 0.0 copy-start.1
  1.3 0.0 copy-start.2
  1.3 0.0 copy-start.3
  1.3 90.4 %shard_map.111 = (f32[96,384]{1,0:T(8,128)S(1)}, f32[1,32]{1,0:T(1,128)S(1)}) custom-call(bf16[2,256,768]{2,1,0:T(8,128)(2,1)} %x0_ref.1, bf16[2,256,768]{2,1,0:T(8,128)(2,1)} %x1_ref.1, bf16[4,4,2,192,256]{4,3,2,1,0:T(8,128)(2,1)} %bitcast.6, bf16[4,4,2,192,256]{4,3,2,1,0:T(8,128)(2,1)} %bitcast.7, s32[1,32]{1,0:T(1,128)S(1)} %bitcast.4), custom_call_target="tpu_custom_call" | custom-call | tf_op jit(solution)/shard_map/pallas_call | solution.py:479
  91.7 0.0 copy-done.1
  91.7 0.0 copy-done.2
  91.7 0.0 copy-done.3
  91.7 0.8 multiply_subtract_fusion
  92.5 0.5 copy.13
Async XLA Ops:
  0.6 0.7 copy-start
  1.3 90.4 %copy-start.1 = (f32[96,384]{1,0:T(8,128)S(1)}, f32[96,384]{1,0:T(8,128)}, u32[]{:S(2)}) copy-start(f32[96,384]{1,0:T(8,128)} %param.13) | copy-start | bytes 442372
  1.3 90.4 %copy-start.2 = (f32[96,384]{1,0:T(8,128)S(1)}, f32[96,384]{1,0:T(8,128)}, u32[]{:S(2)}) copy-start(f32[96,384]{1,0:T(8,128)} %param.14) | copy-start | bytes 442372
  1.3 90.4 %copy-start.3 = (f32[96,384]{1,0:T(8,128)S(1)}, f32[96,384]{1,0:T(8,128)}, u32[]{:S(2)}) copy-start(f32[96,384]{1,0:T(8,128)} %param.15) | copy-start | bytes 442372

commit v7 on v6

--- a/solution.py
+++ b/solution.py
@@ -30,7 +30,7 @@
 def kernel(
     x0_ref, x1_ref, h0_ref, h1_ref, len_ref,
     grad_ref, clip_ref,
-    xb, hb, gall, gs, gr, gh, ys, yr, yhs, yhr, hs, hr, eb, eh, lb, mt, ft, fc, npart, nb, p3,
+    xb, hb, gall, gs, gr, gh, ys, yr, yhs, yhr, hs, hr, eb, eh, lb, mt, ft, fc, npart, nb, p3, xs, hst,
     lsem, llen, sx, sxo, sh, sho, slen, sxf, sn, sg, sy, syh, shh,
     rx, rxo, rh, rho, rlen, rn, rg, ry, ryh, rhh, near,
 ):
@@ -66,14 +66,14 @@
         return gg * 4 + aa if k == 0 else aa * 4 + gg
 
     def h_slice(k, i, aa):
-        return h_refs[k].at[i, aa] if k == 0 else h_refs[k].at[aa, i]
+        return hst.at[k, i, aa] if k == 0 else hst.at[k, aa, i]
 
     def h_all(k, aa):
         return h_refs[k].at[:, aa] if k == 0 else h_refs[k].at[aa]
 
     def d_x(k, s, j):
         gk, ak = place(k)
-        return remote(x_refs[k].at[j], xb.at[c, gk, j], sx.at[k, s, j], rx.at[c, s, j],
+        return remote(xs.at[k, j], xb.at[c, gk, j], sx.at[k, s, j], rx.at[c, s, j],
                       y * 2 + k, mp_k(k, mod4(gk + STEPS[s]), ak))
 
     def d_h(k, s, q):
@@ -122,6 +122,10 @@
     in_x = [mod4(x + s) * 4 + z for s in STEPS[:2]]
     in_z = [x * 4 + mod4(z + s) for s in STEPS[:2]]
     in_y = [mod4(y + s) * 2 for s in STEPS[:2]]
+    staged = [pltpu.make_async_copy(x_refs[k], xs.at[k], lsem.at[2 + k]) for k in range(2)]
+    staged_h = [pltpu.make_async_copy(h_refs[k], hst.at[k], lsem.at[4 + k]) for k in range(2)]
+    for d in staged + staged_h:
+        d.start()
     barrier = pltpu.get_barrier_semaphore()
     signal(barrier, y * 2 + other, mp)
     for k in range(2):
@@ -130,6 +134,8 @@
         for to_dp in in_y:
             signal(barrier, to_dp + k, mp)
     pl.semaphore_wait(barrier, 13)
+    for d in staged:
+        d.wait()
 
     for q in range(2):
         for k in range(2):
@@ -195,6 +201,9 @@
             w_x(cp, s, s)
             d_xf(cp, s).start()
     pl.semaphore_wait(near.at[0], 6)
+    for d in staged_h:
+        d.wait()
+
     def send_rank(*parts):
         for q in parts:
             for s in (2, 0, 1):
@@ -396,6 +405,23 @@
     y_start(*over_high)
     yhr[c, 0] = yhs[dp]
 
+    d_len.wait_send()
+    for k in range(2):
+        @pl.when(c != k)
+        def _():
+            for d in d_own_remote(k):
+                d.wait_send()
+        for s in range(2):
+            for j in range(2):
+                d_x(k, s, j).wait_send()
+            d_xf(k, s).wait_send()
+        for s in range(3):
+            for q in range(5):
+                d_h(k, s, q).wait_send()
+    for q in range(3):
+        for n in range(NEEDED):
+            d_norm(q, n).wait_send()
+
     for n in range(3):
         remote(gr.at[n], gr.at[n], sg.at[n], rg.at[n], dp, mp).wait_recv()
     low = gall[3, :LOW] + gr[0].astype(F32) + gr[1].astype(F32) + gr[2].astype(F32)
@@ -405,6 +431,20 @@
     y_start(*over_low)
     yr[c, 0] = ys[dp]
 
+    def d_high(k, s):
+        gk, ak = place(k)
+        aa = mod4(ak + STEPS[s])
+        return remote(hs.at[k, lax.div(aa, 2)], hr.at[k, s], shh.at[k, s], rhh.at[k, s], dp, mp_k(k, gk, aa))
+
+    y_wait(*over_high)
+    for k in range(2):
+        high = yhr[k, 0].astype(F32)
+        for dy in range(1, 4):
+            high = high + yhr[k, dy].astype(F32)
+        for t in range(2):
+            hs[k, t] = high[:, t * 128 : (t + 1) * 128].astype(BF16)
+        for s in (2, 0, 1):
+            d_high(k, s).start()
     norm_wait(2, NEEDED, ALL)
     rows = nb[2].reshape(32, 128)
     s0, s1 = over_x(rows[:16]), over_z(rows[16:])
@@ -419,21 +459,11 @@
     clip_ref[...] = jnp.sum(
         jnp.where(l32[:, :32] == r32[:, :32], factor(squares), 0.0), axis=0, keepdims=True
     )
-
-    def d_high(k, s):
-        gk, ak = place(k)
-        aa = mod4(ak + STEPS[s])
-        return remote(hs.at[k, lax.div(aa, 2)], hr.at[k, s], shh.at[k, s], rhh.at[k, s], dp, mp_k(k, gk, aa))
-
-    y_wait(*over_high)
-    for k in range(2):
-        high = yhr[k, 0].astype(F32)
-        for dy in range(1, 4):
-            high = high + yhr[k, dy].astype(F32)
-        for t in range(2):
-            hs[k, t] = high[:, t * 128 : (t + 1) * 128].astype(BF16)
-        for s in (2, 0, 1):
-            d_high(k, s).start()
+    for n in range(NEEDED, ALL):
+        d_norm(2, n).wait_send()
+    for n in range(3):
+        d_part(n).wait_send()
+
     total = jnp.dot(hs[0, lax.div(place(0)[1], 2)], eh[0], preferred_element_type=F32)
     total = total + jnp.dot(hs[1, lax.div(place(1)[1], 2)], eh[1], preferred_element_type=F32)
     y_wait(*over_low)
@@ -446,31 +476,14 @@
             total = total + jnp.dot(hr[k, s], eh[k], preferred_element_type=F32)
     grad_ref[...] = total * (1.0 / EXAMPLES)
 
-    d_len.wait_send()
-    for k in range(2):
-        @pl.when(c != k)
-        def _():
-            for d in d_own_remote(k):
-                d.wait_send()
-        for s in range(2):
-            for j in range(2):
-                d_x(k, s, j).wait_send()
-            d_xf(k, s).wait_send()
+    for k in range(2):
         for s in range(3):
-            for q in range(5):
-                d_h(k, s, q).wait_send()
             d_high(k, s).wait_send()
-    for q in range(3):
-        for n in range(NEEDED if q < 2 else ALL):
-            d_norm(q, n).wait_send()
-    for n in range(3):
-        d_part(n).wait_send()
     for refs in (over_low, over_high):
         for dy in (2, 1, 3):
             for k in range(2):
                 d_y(*refs, dy, k).wait_send()
         d_partner(*refs).wait_send()
-
 
 def exchange(layer_input, output_cot, hidden_cot, hidden_act, lengths):
     dma = pltpu.SemaphoreType.DMA
@@ -503,7 +516,9 @@
             pltpu.VMEM((16, 8, 128), F32),
             pltpu.VMEM((3, 32, 1, 128), F32),
             pltpu.VMEM((2, 2, 4, ROWS, D), F32),
-            dma((2,)), dma, dma((2, 2, 2)), dma, dma((2, 3, 5)), dma, dma, dma((2, 2)),
+            pltpu.VMEM((2, 2, SLOT, D), BF16),
+            pltpu.VMEM((2, 4, 4, 2, ROWS, SLOT), BF16),
+            dma((6,)), dma, dma((2, 2, 2)), dma, dma((2, 3, 5)), dma, dma, dma((2, 2)),
             dma((3, 31)), dma((3,)), dma((4, 2)), dma((4, 2)), dma((2, 3)),
             dma((2, 3, 2)), dma, dma((2, 3, 5)), dma, dma, dma((3, 32)), dma((3,)), dma((2, 4)), dma((2, 4)), dma((2, 3)),
             pltpu.SemaphoreType.REGULAR((3,)),

time: 93.1 us -> 92.6 us (level)
  no operation moved by 1% of the time
where the time goes in v7:
time: 92.6 us; the launch traced here: 92.5 us
  Pallas kernels  89.8 us (97%)
  local copies, waits for them, and re-layouts  1.17 us (1%)
    pallas_call x1, Pallas kernels, exchange(): pl.pallas_call(kernel, out_shape=(jax.ShapeDtypeStruct((OWN, 2 * ROWS), F...  89.8 us

profile of v7, /device:TPU:1, one launch (start us, length us, event | category | flops | bytes accessed | tf_op | source)
XLA Modules:
  0.0 92.5 jit_solution(11831571899175291480)
XLA Ops:
  0.6 0.0 copy-start
  0.6 0.6 copy-done
  1.3 0.0 copy-start.1
  1.3 0.0 copy-start.2
  1.3 0.0 copy-start.3
  1.3 89.8 %shard_map.111 = (f32[96,384]{1,0:T(8,128)S(1)}, f32[1,32]{1,0:T(1,128)S(1)}) custom-call(bf16[2,256,768]{2,1,0:T(8,128)(2,1)} %x0_ref.1, bf16[2,256,768]{2,1,0:T(8,128)(2,1)} %x1_ref.1, bf16[4,4,2,192,256]{4,3,2,1,0:T(8,128)(2,1)} %bitcast.6, bf16[4,4,2,192,256]{4,3,2,1,0:T(8,128)(2,1)} %bitcast.7, s32[1,32]{1,0:T(1,128)S(1)} %bitcast.4), custom_call_target="tpu_custom_call" | custom-call | tf_op jit(solution)/shard_map/pallas_call | solution.py:492
  91.1 0.0 copy-done.1
  91.1 0.0 copy-done.2
  91.1 0.0 copy-done.3
  91.1 0.8 multiply_subtract_fusion
  92.0 0.5 copy.13
Async XLA Ops:
  0.6 0.7 copy-start
  1.3 89.8 %copy-start.1 = (f32[96,384]{1,0:T(8,128)S(1)}, f32[96,384]{1,0:T(8,128)}, u32[]{:S(2)}) copy-start(f32[96,384]{1,0:T(8,128)} %param.13) | copy-start | bytes 442372
  1.3 89.8 %copy-start.2 = (f32[96,384]{1,0:T(8,128)S(1)}, f32[96,384]{1,0:T(8,128)}, u32[]{:S(2)}) copy-start(f32[96,384]{1,0:T(8,128)} %param.14) | copy-start | bytes 442372
  1.3 89.8 %copy-start.3 = (f32[96,384]{1,0:T(8,128)S(1)}, f32[96,384]{1,0:T(8,128)}, u32[]{:S(2)}) copy-start(f32[96,384]{1,0:T(8,128)} %param.15) | copy-start | bytes 442372

commit v8 on v7

--- a/solution.py
+++ b/solution.py
@@ -466,14 +466,18 @@
 
     total = jnp.dot(hs[0, lax.div(place(0)[1], 2)], eh[0], preferred_element_type=F32)
     total = total + jnp.dot(hs[1, lax.div(place(1)[1], 2)], eh[1], preferred_element_type=F32)
+    def spread(blocks, count, table):
+        out = jnp.dot(blocks.reshape(count * OWN, 128), table, preferred_element_type=F32)
+        return sum(out[n * OWN : (n + 1) * OWN] for n in range(1, count)) + out[:OWN]
+
     y_wait(*over_low)
     for k in range(2):
-        for dy in range(4):
-            total = total + jnp.dot(yr[k, dy], eb[k], preferred_element_type=F32)
+        total = total + spread(yr[k], 4, eb[k])
     for k in range(2):
         for s in (0, 1, 2):
             remote(hr.at[k, s], hr.at[k, s], shh.at[k, s], rhh.at[k, s], dp, mp).wait_recv()
-            total = total + jnp.dot(hr[k, s], eh[k], preferred_element_type=F32)
+    for k in range(2):
+        total = total + spread(hr[k], 3, eh[k])
     grad_ref[...] = total * (1.0 / EXAMPLES)
 
     for k in range(2):

time: 92.6 us -> 92.4 us (level)
  no operation moved by 1% of the time
where the time goes in v8:
time: 92.4 us; the launch traced here: 92.3 us
  Pallas kernels  89.6 us (97%)
  local copies, waits for them, and re-layouts  1.17 us (1%)
    pallas_call x1, Pallas kernels, exchange(): pl.pallas_call(kernel, out_shape=(jax.ShapeDtypeStruct((OWN, 2 * ROWS), F...  89.6 us

profile of v8, /device:TPU:1, one launch (start us, length us, event | category | flops | bytes accessed | tf_op | source)
XLA Modules:
  0.0 92.3 jit_solution(14047320541838931089)
XLA Ops:
  0.6 0.0 copy-start
  0.6 0.6 copy-done
  1.3 0.0 copy-start.1
  1.3 0.0 copy-start.2
  1.3 0.0 copy-start.3
  1.3 89.6 %shard_map.111 = (f32[96,384]{1,0:T(8,128)S(1)}, f32[1,32]{1,0:T(1,128)S(1)}) custom-call(bf16[2,256,768]{2,1,0:T(8,128)(2,1)} %x0_ref.1, bf16[2,256,768]{2,1,0:T(8,128)(2,1)} %x1_ref.1, bf16[4,4,2,192,256]{4,3,2,1,0:T(8,128)(2,1)} %bitcast.6, bf16[4,4,2,192,256]{4,3,2,1,0:T(8,128)(2,1)} %bitcast.7, s32[1,32]{1,0:T(1,128)S(1)} %bitcast.4), custom_call_target="tpu_custom_call" | custom-call | tf_op jit(solution)/shard_map/pallas_call | solution.py:496
  90.9 0.0 copy-done.1
  90.9 0.0 copy-done.2
  90.9 0.0 copy-done.3
  90.9 0.8 multiply_subtract_fusion
  91.8 0.5 copy.13
Async XLA Ops:
  0.6 0.7 copy-start
  1.3 89.6 %copy-start.1 = (f32[96,384]{1,0:T(8,128)S(1)}, f32[96,384]{1,0:T(8,128)}, u32[]{:S(2)}) copy-start(f32[96,384]{1,0:T(8,128)} %param.13) | copy-start | bytes 442372
  1.3 89.6 %copy-start.2 = (f32[96,384]{1,0:T(8,128)S(1)}, f32[96,384]{1,0:T(8,128)}, u32[]{:S(2)}) copy-start(f32[96,384]{1,0:T(8,128)} %param.14) | copy-start | bytes 442372
  1.3 89.6 %copy-start.3 = (f32[96,384]{1,0:T(8,128)S(1)}, f32[96,384]{1,0:T(8,128)}, u32[]{:S(2)}) copy-start(f32[96,384]{1,0:T(8,128)} %param.15) | copy-start | bytes 442372
